TPU v7x, 8 devices: a whole 2x2x1 slice. The times are simulated.
8 devices in a mesh: b: 2 (over z, y), a: 4 (over x, core).
Axes of the slice: x: 2, y: 2, z: 1, core: 2. Of those that a mesh axis runs over, the one named last changes fastest.
Arguments:
- u: float32 [256, 256, 256], P(None, 'a', 'b')
- g: float32 [132, 256, 256], P('a', 'b')
Outputs:
- output: float32 [256, 256, 256], P(None, 'a', 'b')
All inputs are finite; a program needn't handle non-finite values.
Results may differ from a plain program's by a relative error of at most 0.001.
Values are sent between devices in bfloat16 or wider.
A program may use at most 1 GiB of HBM per device.

v0:
```python
import math
import functools
import jax
import jax.numpy as jnp
from jax import lax
from jax.sharding import PartitionSpec as P

HI = lax.Precision.HIGHEST


def _trig(n, rows, cols):
    r = jnp.arange(rows, dtype=jnp.int32)[:, None]
    c = jnp.arange(cols, dtype=jnp.int32)[None, :]
    ang = ((r * c) % n).astype(jnp.float32) * (2.0 * math.pi / n)
    return jnp.cos(ang), jnp.sin(ang)


def _xtables(n, kx):
    cx, sx = _trig(n, kx, n)
    k = jnp.arange(kx)
    keep = (k <= n // 2).astype(jnp.float32)
    wgt = jnp.where((k == 0) | (k == n // 2), 1.0, 2.0) * keep / n
    return cx * keep[:, None], -sx * keep[:, None], (cx * wgt[:, None]).T, (sx * wgt[:, None]).T


def _mm(p, q):
    return jnp.dot(p, q, precision=HI, preferred_element_type=jnp.float32)


def _line(x, c, s, form, sign):
    e = functools.partial(jnp.einsum, form, precision=HI, preferred_element_type=jnp.float32)
    return jnp.stack([e(x[0], c) + sign * e(x[1], s), e(x[1], c) - sign * e(x[0], s)])


def solution(mesh):
    na = mesh.shape["a"]

    def local(u, g):
        n, ya, zb = u.shape
        kx = g.shape[0] * na
        c1, s1, ar, ai = _xtables(n, kx)
        c, s = _trig(n, n, n)
        ci, si = c / n, s / n
        u2 = u.reshape(n, ya * zb)
        x = jnp.stack([_mm(c1, u2), _mm(s1, u2)]).reshape(2, kx, ya, zb)
        x = lax.all_to_all(x, "a", 1, 2, tiled=True)
        x = _line(x, c, s, "xyz,yk->xkz", 1.0)
        x = lax.all_to_all(x, "b", 2, 3, tiled=True)
        x = _line(x, c, s, "xyz,zk->xyk", 1.0) * g[None]
        x = _line(x, ci, si, "xyz,zk->xyk", -1.0)
        x = lax.all_to_all(x, "b", 3, 2, tiled=True)
        x = _line(x, ci, si, "xyz,yk->xkz", -1.0)
        x = lax.all_to_all(x, "a", 2, 1, tiled=True)
        w = _mm(ar, x[0].reshape(kx, ya * zb)) - _mm(ai, x[1].reshape(kx, ya * zb))
        return w.reshape(n, ya, zb)

    return jax.shard_map(local, mesh=mesh, in_specs=(P(None, "a", "b"), P("a", "b", None)), out_specs=P(None, "a", "b"), check_vma=False)
```

profile of v0, /device:TPU:0, one launch (start us, length us, event | category | flops | bytes accessed | tf_op | source)
XLA Modules:
  0.0 698.0 jit_solution(1571876036344442270)
XLA Ops:
  0.0 14.4 %copy.98 = f32[32,8,64,128]{3,1,2,0:T(8,128)} copy(f32[32,8,64,128]{3,2,1,0:T(8,128)} %bitcast.173) | data formatting | bytes 16777216
  14.4 9.4 %copy.54 = f32[8192,256]{1,0:T(8,128)} copy(f32[8192,256]{0,1:T(8,128)} %bitcast.166) | data formatting | bytes 16777216 | tf_op jit(solution)/shard_map/dot_general | solution.py:27
  23.8 12.9 %convolution_bitcast_fusion = f32[1,132,64,128]{3,1,2,0:T(8,128)S(1)} fusion(f32[64,128,256]{2,1,0:T(8,128)} %bitcast.146, f32[132]{0:T(256)S(1)} %fusion.99), kind=kOutput, calls=%fused_computation.24 | convolution fusion | flops 3322429440 | bytes 12714512 | tf_op jit(solution)/shard_map/dot_general | solution.py:27
  36.8 9.5 %convolution_bitcast_fusion.1 = f32[1,132,64,128]{3,1,2,0:T(8,128)S(1)} fusion(f32[64,128,256]{2,1,0:T(8,128)S(1)} %bitcast.147, f32[132]{0:T(256)S(1)} %fusion.99), kind=kOutput, calls=%fused_computation.25 | convolution fusion | flops 3322395648 | bytes 12714512 | tf_op jit(solution)/shard_map/dot_general | solution.py:27
  48.5 100.7 %all_to_all.60 = f32[2,132,64,128]{3,2,0,1:T(8,128)} all-to-all(f32[2,132,64,128]{3,2,0,1:T(8,128)S(1)} %copy.55), channel_id=1, replica_groups=mesh['b'=2,'a'=4] {'a'}, dimensions={1} | all-to-all | bytes 17301504 | tf_op jit(solution)/shard_map/all_to_all | solution.py:46
  155.9 5.0 fusion.22
  161.4 5.2 fusion.20
  166.6 5.6 add_bitcast_fusion.3
  172.2 5.6 subtract_bitcast_fusion.3
  178.9 35.2 %copy.59 = f32[2,33,256,128]{3,0,1,2:T(2,128)S(1)} copy(f32[2,33,256,128]{3,2,1,0:T(8,128)S(1)} %pad_maximum_fusion.1) | data formatting | bytes 17301504 | tf_op jit(solution)/shard_map/stack | solution.py:32
  214.0 98.6 %all_to_all.61 = f32[2,33,256,128]{3,0,1,2:T(2,128)S(1)} all-to-all(f32[2,33,256,128]{3,0,1,2:T(2,128)S(1)} %copy.59), channel_id=1, replica_groups=mesh['b'=2,'a'=4] {'b'}, dimensions={2} | all-to-all | bytes 17301504 | tf_op jit(solution)/shard_map/all_to_all | solution.py:48
  312.6 8.4 %copy.97 = f32[2,33,2,128,128]{4,2,3,1,0:T(2,128)} copy(f32[2,33,2,128,128]{4,0,1,3,2:T(2,128)S(1)} %bitcast.164) | data formatting | bytes 17301504 | tf_op jit(solution)/shard_map/all_to_all | solution.py:48
  321.0 8.0 %fusion.194 = (f32[1,33,128,2,128]{4,3,2,1,0:T(2,128)}, f32[1,33,128,2,128]{4,3,2,1,0:T(2,128)}) fusion(f32[2,33,128,2,128]{4,3,2,1,0:T(2,128)} %bitcast.161), kind=kLoop, calls=%fused_computation.207 | loop fusion | bytes 17301504 | tf_op jit(solution)/shard_map/slice | solution.py:32
  329.1 6.5 squeeze.34
  335.6 6.5 squeeze.35
  342.1 7.6 %fusion.16 = f32[33,128,256]{2,1,0:T(8,128)S(1)} fusion(f32[33,128,256]{2,1,0:T(8,128)} %squeeze.35), kind=kOutput, calls=%fused_computation.40 | convolution fusion | flops 3322806272 | bytes 8650752 | tf_op jit(solution)/shard_map/xyz,zk->xyk/dot_general | solution.py:32
  354.4 4.9 subtract_bitcast_fusion.2
  359.3 5.1 add_bitcast_fusion.2
  375.5 5.3 subtract_bitcast_fusion.1
  389.8 13.9 %copy.69 = f32[2,33,128,256]{2,0,1,3:T(2,128)} copy(f32[2,33,128,256]{3,2,1,0:T(8,128)} %pad_maximum_fusion.2) | data formatting | bytes 17301504 | tf_op jit(solution)/shard_map/stack | solution.py:32
  403.7 105.4 %all_to_all.62 = f32[2,33,128,256]{2,0,1,3:T(2,128)} all-to-all(f32[2,33,128,256]{2,0,1,3:T(2,128)} %copy.69), channel_id=1, replica_groups=mesh['b'=2,'a'=4] {'b'}, dimensions={3} | all-to-all | bytes 17301504 | tf_op jit(solution)/shard_map/all_to_all | solution.py:51
  509.1 14.3 %copy.70 = f32[2,33,128,2,128]{4,2,3,1,0:T(8,128)} copy(f32[2,33,128,2,128]{2,0,1,4,3:T(2,128)} %bitcast.165) | data formatting | bytes 17301504 | tf_op jit(solution)/shard_map/all_to_all | solution.py:51
  527.6 5.0 fusion.26
  532.7 5.0 fusion.28
  537.7 5.9 subtract_bitcast_fusion
  543.6 5.7 add_bitcast_fusion
  550.3 10.4 %copy.71 = f32[2,33,256,128]{3,0,1,2:T(2,128)} copy(f32[2,33,256,128]{3,2,1,0:T(8,128)S(1)} %pad_maximum_fusion.3) | data formatting | bytes 17301504 | tf_op jit(solution)/shard_map/stack | solution.py:32
  560.7 6.1 all-to-all-start.3
  566.8 95.2 %all-to-all-done.3 = f32[2,33,256,128]{3,0,1,2:T(2,128)} async-done(((f32[2,33,256,128]{3,0,1,2:T(2,128)}), f32[2,33,256,128]{3,0,1,2:T(2,128)}, u32[]{:S(2)}, u32[]{:S(2)}) %all-to-all-start.3) | async-done | bytes 8650784 | tf_op jit(solution)/shard_map/all_to_all | solution.py:53
  676.2 8.1 %fusion.58 = f32[256,8192]{1,0:T(8,128)S(1)} fusion(f32[132,8192]{1,0:T(8,128)S(1)} %bitcast.170, f32[132]{0:T(256)S(1)} %fusion.103), kind=kOutput, calls=%fused_computation.88 | convolution fusion | flops 3322395648 | bytes 12714512 | tf_op jit(solution)/shard_map/dot_general | solution.py:27
  684.3 8.4 %fusion.4 = f32[32,8,64,128]{3,1,2,0:T(8,128)S(1)} fusion(f32[256,8192]{1,0:T(8,128)S(1)} %fusion.58, f32[132,8192]{1,0:T(8,128)S(1)} %bitcast.167, f32[132]{0:T(256)S(1)} %fusion.103), kind=kOutput, calls=%fused_computation.23 | convolution fusion | flops 3324492800 | bytes 21103120 | tf_op jit(solution)/shard_map/dot_general | solution.py:27
  692.7 5.0 copy.92
  (40 shorter events, 54.4 us)
Async XLA Ops:
  23.8 12.9 %copy-start = (f32[8192,256]{1,0:T(8,128)S(1)}, f32[8192,256]{1,0:T(8,128)}, u32[]{:S(2)}) copy-start(f32[8192,256]{1,0:T(8,128)} %copy.54) | copy-start | bytes 25165828
  335.6 14.2 %slice-start = ((s8[4325376]{0:T(1024)(128)(4,1)}), s8[131072]{0:T(1024)(128)(4,1)S(1)}, s32[]{:S(2)}) async-start(s8[4325376]{0:T(1024)(128)(4,1)} %bitcast.152), calls=%async_computation.4 | async-start | bytes 262144
  342.1 7.7 %slice-start.1 = ((s8[4325376]{0:T(1024)(128)(4,1)}), s8[4194304]{0:T(1024)(128)(4,1)S(1)}, s32[]{:S(2)}) async-start(s8[4325376]{0:T(1024)(128)(4,1)} %bitcast.152), calls=%async_computation.5 | async-start | bytes 8388608
  349.8 9.5 %slice-start.2 = ((s8[4325376]{0:T(1024)(128)(4,1)}), s8[4194304]{0:T(1024)(128)(4,1)S(1)}, s32[]{:S(2)}) async-start(s8[4325376]{0:T(1024)(128)(4,1)} %bitcast.154), calls=%async_computation.6 | async-start | bytes 8388608
  354.3 4.9 slice-start.3
  354.4 10.1 %slice-start.4 = ((s8[4325376]{0:T(1024)(128)(4,1)}), s8[4194304]{0:T(1024)(128)(4,1)S(1)}, s32[]{:S(2)}) async-start(s8[4325376]{0:T(1024)(128)(4,1)} %bitcast.174), calls=%async_computation.8 | async-start | bytes 8388608
  359.3 5.1 slice-start.5
  560.7 101.3 %all-to-all-start.3 = ((f32[2,33,256,128]{3,0,1,2:T(2,128)}), f32[2,33,256,128]{3,0,1,2:T(2,128)}, u32[]{:S(2)}, u32[]{:S(2)}) async-start(f32[2,33,256,128]{3,0,1,2:T(2,128)} %copy.71), calls=%async_computation.3 | async-start | bytes 17301504 | tf_op jit(solution)/shard_map/all_to_all | solution.py:53
where the time goes:
time: 705 us; the launch traced here: 698 us
  blocking collectives  305 us (43%)
  local copies, waits for them, and re-layouts  159 us (23%)
  matrix products  123 us (17%)
  waiting for transfers between devices  95.2 us (14%)
  other arithmetic  8.71 us (1%)
    all_to_all x1, blocking collectives, local(): x = lax.all_to_all(x, 'b', 3, 2, tiled=True)  105 us
    all_to_all x1, blocking collectives, local(): x = lax.all_to_all(x, 'a', 1, 2, tiled=True)  101 us
    all_to_all x1, blocking collectives, local(): x = lax.all_to_all(x, 'b', 2, 3, tiled=True)  98.6 us
    all_to_all x1, waiting for transfers between devices, local(): x = lax.all_to_all(x, 'a', 2, 1, tiled=True)  95.2 us
    another operation x3, local copies, waits for them, and re-layouts, _line(): jnp.stack([e(x[0], c) + sign * e(x[1], s), e(x[1], c) - sign * e(x[0], s)])  59.4 us
    dot_general x4, matrix products, _mm(): return jnp.dot(p, q, precision=HI, preferred_element_type=jnp.float32)  38.9 us
    unnamed x20, local copies, waits for them, and re-layouts  27.3 us
    dot_general x4, matrix products, _line(): e(x[1], c) - sign * e(x[0], s)  23.1 us
  transfers between devices with their start and end apart: 1, of which 1 were waited for; matrix products, arithmetic and copies ran while one was open for 0% of the time, Pallas kernels for 0%

commit v1 on v0

v1 whole, which is shorter than its diff:
```python
import functools
import math

import jax
import jax.numpy as jnp
import numpy as np
from jax import lax
from jax.experimental import pallas as pl
from jax.experimental.pallas import tpu as pltpu
from jax.sharding import PartitionSpec as P

N = 256
H = 128
KB = 33
NA = 4
NB = 2
YA = 64
CH = 3
NCH = KB // CH
F32 = jnp.float32
BF16 = jnp.bfloat16
MESH = pl.DeviceIdType.MESH


def _np_split(x):
    x = np.asarray(x, np.float32)
    out = []
    for _ in range(3):
        p = x.astype(jnp.bfloat16)
        out.append(p)
        x = x - p.astype(np.float32)
    return np.stack(out)


def _np_tables():
    r = np.arange(N)
    ang = ((r[:, None] * r[None, :]) % N).astype(np.float32) * np.float32(2.0 * math.pi / N)
    c = np.cos(ang.astype(np.float64)).astype(np.float32)
    s = np.sin(ang.astype(np.float64)).astype(np.float32)
    cs = np.stack([_np_split(c), _np_split(s)], 1)
    t1 = np.concatenate([c[:H + 1], -s[1:H]], 0)
    wgt = np.where((r == 0) | (r == H), 1.0, 2.0).astype(np.float32) / N
    t5 = np.concatenate([c[:, :H + 1] * wgt[:H + 1], -s[:, 1:H] * wgt[1:H]], 1)
    return cs, _np_split(t1), _np_split(t5)


def _split(x):
    h = x.astype(BF16)
    r = x - h.astype(F32)
    m = r.astype(BF16)
    return h, m, (r - m.astype(F32)).astype(BF16)


PAIRS = ((0, 0), (0, 1), (1, 0), (1, 1), (0, 2), (2, 0))


def _dot6(ls, rs):
    acc = None
    for i, j in PAIRS:
        d = jnp.dot(ls[i], rs[j], preferred_element_type=F32)
        acc = d if acc is None else acc + d
    return acc


def _k0(t_ref, u_ref, o_ref):
    t = jnp.swapaxes(u_ref[...], 0, 1)
    tab = [t_ref[p] for p in range(3)]
    res, ims = [], []
    for j in range(4):
        x = jnp.concatenate([t[2 * j], t[2 * j + 1]], axis=1)
        acc = _dot6(tab, _split(x))
        res += [acc[:H, :H], acc[:H, H:]]
        ims += [acc[H:, :H], acc[H:, H:]]
    re = jnp.swapaxes(jnp.stack(res), 0, 1)
    im = jnp.swapaxes(jnp.stack(ims), 0, 1)
    z = jnp.zeros((1, 8, H), F32)
    o_ref[:H, :, :H] = re
    o_ref[0:1, :, H:] = z
    o_ref[1:H, :, H:] = im[1:]
    o_ref[H:H + 1, :, :H] = im[0:1]
    o_ref[H:H + 1, :, H:] = z
    o_ref[H + 1:, :, :] = jnp.zeros((NA * KB - H - 1, 8, N), F32)


def _k2(t_ref, v_ref, o_ref):
    re = jnp.swapaxes(v_ref[:H, :, :H], 0, 1)
    im = jnp.swapaxes(jnp.concatenate([v_ref[H:H + 1, :, :H], v_ref[1:H, :, H:]], 0), 0, 1)
    tab = [t_ref[p] for p in range(3)]
    outs = []
    for j in range(4):
        x = jnp.concatenate([
            jnp.concatenate([re[2 * j], re[2 * j + 1]], axis=1),
            jnp.concatenate([im[2 * j], im[2 * j + 1]], axis=1)], axis=0)
        acc = _dot6(tab, _split(x))
        outs += [acc[:, :H], acc[:, H:]]
    o_ref[...] = jnp.swapaxes(jnp.stack(outs), 0, 1)


def _k1(cs_ref, xs_ref, g_ref, v_ref, r1, y2, r2, r3, gv, w3, w3i, t4,
        s1, q1, l1, s2, q2, s3, q3, s4, q4, l4, gsem):
    a = lax.axis_index("a")
    b = lax.axis_index("b")
    ob = 1 - b

    barrier = pltpu.get_barrier_semaphore()
    for d in range(1, NA):
        pl.semaphore_signal(barrier, inc=1, device_id=(b, lax.rem(a + d, NA)), device_id_type=MESH)
    pl.semaphore_signal(barrier, inc=1, device_id=(ob, a), device_id_type=MESH)
    pl.semaphore_wait(barrier, NA)

    def rows(blk):
        return pl.ds(pl.multiple_of(blk * YA, YA), YA)

    def planes(c):
        return pl.ds(c * CH, CH)

    own = pl.ds(pl.multiple_of(b * H, H), H)
    oth = pl.ds(pl.multiple_of(ob * H, H), H)

    def e1(c, d, to, frm):
        return pltpu.make_async_remote_copy(
            src_ref=xs_ref.at[pl.ds(to * KB + c * CH, CH)],
            dst_ref=r1.at[planes(c), rows(frm)],
            send_sem=s1.at[c, d - 1], recv_sem=q1.at[c, d - 1],
            device_id=(b, to), device_id_type=MESH)

    def e1_own(c):
        return pltpu.make_async_copy(
            xs_ref.at[pl.ds(a * KB + c * CH, CH)], r1.at[planes(c), rows(a)], l1.at[c])

    def e2(c):
        return pltpu.make_async_remote_copy(
            src_ref=y2.at[planes(c), oth], dst_ref=r2.at[planes(c)],
            send_sem=s2.at[c], recv_sem=q2.at[c], device_id=(ob, a), device_id_type=MESH)

    def e3(c):
        return pltpu.make_async_remote_copy(
            src_ref=r2.at[planes(c)], dst_ref=r3.at[planes(c)],
            send_sem=s3.at[c], recv_sem=q3.at[c], device_id=(ob, a), device_id_type=MESH)

    def e4(c, d, to, frm):
        return pltpu.make_async_remote_copy(
            src_ref=r1.at[planes(c), rows(to)],
            dst_ref=v_ref.at[pl.ds(frm * KB + c * CH, CH)],
            send_sem=s4.at[c, d - 1], recv_sem=q4.at[c, d - 1],
            device_id=(b, to), device_id_type=MESH)

    def e4_own(c):
        return pltpu.make_async_copy(
            r1.at[planes(c), rows(a)], v_ref.at[pl.ds(a * KB + c * CH, CH)], l4.at[c])

    gcopy = pltpu.make_async_copy(g_ref, gv, gsem)

    @pl.loop(0, NCH)
    def _(c):
        for d in (2, 1, 3):
            e1(c, d, lax.rem(a + d, NA), a).start()
        e1_own(c).start()

    gcopy.start()

    for p in range(3):
        for k, sl in ((0, own), (1, oth)):
            cr, sr = cs_ref[p, 0, sl, :], cs_ref[p, 1, sl, :]
            w3[p, k * N:k * N + H, :N] = cr
            w3[p, k * N:k * N + H, N:] = -sr
            w3[p, k * N + H:(k + 1) * N, :N] = sr
            w3[p, k * N + H:(k + 1) * N, N:] = cr
            cc = (cs_ref[p, 0, :, sl].astype(F32) * (1.0 / N)).astype(BF16)
            sc = (cs_ref[p, 1, :, sl].astype(F32) * (1.0 / N)).astype(BF16)
            w3i[p, :N, k * N:k * N + H] = cc
            w3i[p, :N, k * N + H:(k + 1) * N] = sc
            w3i[p, N:, k * N:k * N + H] = -sc
            w3i[p, N:, k * N + H:(k + 1) * N] = cc
            t4[p, :N, k * H:(k + 1) * H] = cc
            t4[p, N:, k * H:(k + 1) * H] = sc

    def stage2(c):
        for d in (2, 1, 3):
            frm = lax.rem(a + NA - d, NA)
            e1(c, d, frm, frm).wait_recv()
        e1_own(c).wait()

        @pl.loop(0, CH)
        def _(p):
            k = c * CH + p
            acc = _dot6([cs_ref[q].reshape(2 * N, N) for q in range(3)], _split(r1[k]))
            y2[k, :, :H] = acc[:N, :H] + acc[N:, H:]
            y2[k, :, H:] = acc[:N, H:] - acc[N:, :H]

        e2(c).start()

    def stage3(c):
        e2(c).wait_recv()

        @pl.loop(0, CH)
        def _(p):
            k = c * CH + p
            x = _split(jnp.concatenate([y2[k, own, :], r2[k]], axis=1))
            z = _dot6(x, [w3[q] for q in range(3)])
            gk = gv[k]
            z = _split(jnp.concatenate([z[:, :N] * gk, z[:, N:] * gk], axis=1))
            z = _dot6(z, [w3i[q] for q in range(3)])
            y2[k, own, :] = z[:, :N]
            r2[k] = z[:, N:]

        e3(c).start()

    def stage4(c):
        e3(c).wait_recv()

        @pl.loop(0, CH)
        def _(p):
            k = c * CH + p
            x = jnp.concatenate([y2[k, own, :], r3[k]], axis=0)
            acc = _dot6([t4[q] for q in range(3)], _split(x))
            r1[k, :, :H] = acc[:N, :H] - acc[N:, H:]
            r1[k, :, H:] = acc[:N, H:] + acc[N:, :H]

        for d in (2, 1, 3):
            e4(c, d, lax.rem(a + d, NA), a).start()
        e4_own(c).start()

    gcopy.wait()

    @pl.loop(0, NCH + 2)
    def _(i):
        @pl.when(i < NCH)
        def _():
            stage2(i)

        @pl.when(jnp.logical_and(i >= 1, i <= NCH))
        def _():
            stage3(i - 1)

        @pl.when(i >= 2)
        def _():
            stage4(i - 2)

    @pl.loop(0, NCH)
    def _(c):
        for d in range(1, NA):
            frm = lax.rem(a + NA - d, NA)
            to = lax.rem(a + d, NA)
            e1(c, d, to, a).wait_send()
            e4(c, d, to, a).wait_send()
            e4(c, d, frm, frm).wait_recv()
        e2(c).wait_send()
        e3(c).wait_send()
        e4_own(c).wait()


def solution(mesh):
    cs_np, t1_np, t5_np = _np_tables()
    dma = pltpu.SemaphoreType.DMA

    def local(u, g):
        cs, t1, t5 = jnp.asarray(cs_np), jnp.asarray(t1_np), jnp.asarray(t5_np)
        full = pl.BlockSpec((3, N, N), lambda i: (0, 0, 0))
        params = pltpu.CompilerParams(vmem_limit_bytes=60 * 2**20)
        xs = pl.pallas_call(
            _k0, grid=(YA // 8,), name="fwd_x",
            in_specs=[full, pl.BlockSpec((N, 8, H), lambda i: (0, i, 0))],
            out_specs=pl.BlockSpec((NA * KB, 8, N), lambda i: (0, i, 0)),
            out_shape=jax.ShapeDtypeStruct((NA * KB, YA, N), F32),
            compiler_params=params,
        )(t1, u)
        v = pl.pallas_call(
            _k1, name="yz",
            in_specs=[pl.BlockSpec(memory_space=pltpu.VMEM), pl.BlockSpec(memory_space=pl.ANY),
                      pl.BlockSpec(memory_space=pl.ANY)],
            out_specs=pl.BlockSpec(memory_space=pl.ANY),
            out_shape=jax.ShapeDtypeStruct((NA * KB, YA, N), F32),
            scratch_shapes=[
                pltpu.VMEM((KB, N, N), F32), pltpu.VMEM((KB, N, N), F32),
                pltpu.VMEM((KB, H, N), F32), pltpu.VMEM((KB, H, N), F32),
                pltpu.VMEM((KB, H, N), F32),
                pltpu.VMEM((3, 2 * N, 2 * N), BF16), pltpu.VMEM((3, 2 * N, 2 * N), BF16),
                pltpu.VMEM((3, 2 * N, N), BF16),
                dma((NCH, 3)), dma((NCH, 3)), dma((NCH,)),
                dma((NCH,)), dma((NCH,)), dma((NCH,)), dma((NCH,)),
                dma((NCH, 3)), dma((NCH, 3)), dma((NCH,)), dma,
            ],
            compiler_params=pltpu.CompilerParams(
                collective_id=0, has_side_effects=True, vmem_limit_bytes=60 * 2**20),
        )(cs, xs, g)
        return pl.pallas_call(
            _k2, grid=(YA // 8,), name="inv_x",
            in_specs=[full, pl.BlockSpec((NA * KB, 8, N), lambda i: (0, i, 0))],
            out_specs=pl.BlockSpec((N, 8, H), lambda i: (0, i, 0)),
            out_shape=jax.ShapeDtypeStruct((N, YA, H), F32),
            compiler_params=params,
        )(t5, v)

    return jax.shard_map(local, mesh=mesh, in_specs=(P(None, "a", "b"), P("a", "b", None)),
                         out_specs=P(None, "a", "b"), check_vma=False)
```

time: 705 us -> 246 us (0.35)
  blocking collectives: 305 us -> 0 us
  Pallas kernels: 0 us -> 245 us
  local copies, waits for them, and re-layouts: 159 us -> 0 us
  matrix products: 123 us -> 0 us
  waiting for transfers between devices: 95.2 us -> 0 us
  other arithmetic: 8.71 us -> 0 us
    all_to_all x3 -> x0, blocking collectives: 305 us -> none  [the longest x1 105 us: local(): x = lax.all_to_all(x, 'b', 3, 2, tiled=True)]
    pallas_call x0 -> x3, Pallas kernels: none -> 245 us  [the longest x1 218 us: local(): pl.pallas_call(_k1, name='yz', in_specs=[pl.BlockSpec(memory_space=pltpu....]
    dot_general x20 -> x0, matrix products: 123 us -> none  [the longest x4 38.9 us: _mm(): return jnp.dot(p, q, precision=HI, preferred_element_type=jnp.float32)]
    all_to_all x1 -> x0, waiting for transfers between devices: 95.2 us -> none  [local(): x = lax.all_to_all(x, 'a', 2, 1, tiled=True)]
    another operation x4 -> x0, local copies, waits for them, and re-layouts: 61.1 us -> none  [the longest x3 59.4 us: _line(): jnp.stack([e(x[0], c) + sign * e(x[1], s), e(x[1], c) - sign * e(x[0], s)])]
    all_to_all x4 -> x0, local copies, waits for them, and re-layouts: 31.8 us -> none  [the longest x1 14.3 us: local(): x = lax.all_to_all(x, 'b', 3, 2, tiled=True)]
    unnamed x20 -> x0, local copies, waits for them, and re-layouts: 27.3 us -> none
    slice x6 -> x0, local copies, waits for them, and re-layouts: 16.8 us -> none  [the longest x4 14.5 us: _line(): x[0]]
  transfers between devices with their start and end apart: 1 -> 0, of which waited for: 1 -> 0; matrix products, arithmetic and copies ran while one was open for 0% -> 0% of each run, Pallas kernels for 0% -> 0%
where the time goes in v1:
time: 246 us; the launch traced here: 245 us
  Pallas kernels  245 us (100%)
    pallas_call x1, Pallas kernels, local(): pl.pallas_call(_k1, name='yz', in_specs=[pl.BlockSpec(memory_space=pltpu....  218 us
    pallas_call x1, Pallas kernels, local(): pl.pallas_call(_k2, grid=(YA // 8,), name='inv_x', in_specs=[full, pl.Blo...  13.4 us
    pallas_call x1, Pallas kernels, local(): pl.pallas_call(_k0, grid=(YA // 8,), name='fwd_x', in_specs=[full, pl.Blo...  13.2 us

profile of v1, /device:TPU:0, one launch (start us, length us, event | category | flops | bytes accessed | tf_op | source)
XLA Modules:
  0.0 245.1 jit_solution(13775568451975334647)
XLA Ops:
  0.0 13.2 %fwd_x.1.xs_ref = f32[132,64,256]{2,1,0:T(8,128)} custom-call(bf16[3,256,256]{2,1,0:T(8,128)(2,1)} %constant.7.clone.t_ref, f32[256,64,128]{2,1,0:T(8,128)} %u_ref.1), custom_call_target="tpu_custom_call" | custom-call | tf_op jit(solution)/shard_map/fwd_x/pallas_call | solution.py:261
  13.2 218.5 %yz.1.v_ref = f32[132,64,256]{2,1,0:T(8,128)} custom-call(bf16[3,2,256,256]{3,2,1,0:T(8,128)(2,1)} %constant.6.clone.cs_ref, f32[132,64,256]{2,1,0:T(8,128)} %fwd_x.1.xs_ref, f32[33,128,256]{2,1,0:T(8,128)} %g_ref.1), custom_call_target="tpu_custom_call" | custom-call | tf_op jit(solution)/shard_map/yz/pallas_call | solution.py:268
  231.7 13.4 %inv_x.1 = f32[256,64,128]{2,1,0:T(8,128)} custom-call(bf16[3,256,256]{2,1,0:T(8,128)(2,1)} %constant.8.clone.t_ref, f32[132,64,256]{2,1,0:T(8,128)} %yz.1.v_ref), custom_call_target="tpu_custom_call" | custom-call | tf_op jit(solution)/shard_map/inv_x/pallas_call | solution.py:287

commit v2 on v1

v2 whole, which is shorter than its diff:
```python
import functools
import math

import jax
import jax.numpy as jnp
import numpy as np
from jax import lax
from jax.experimental import pallas as pl
from jax.experimental.pallas import tpu as pltpu
from jax.sharding import PartitionSpec as P

N = 256
H = 128
KB = 33
NA = 4
NB = 2
YA = 64
G = 8
NG = YA // G
US = 4
EARLY = 2
A2 = 2
A3 = 2
F32 = jnp.float32
BF16 = jnp.bfloat16
MESH = pl.DeviceIdType.MESH


def _np_split(x):
    x = np.asarray(x, np.float32)
    out = []
    for _ in range(3):
        p = x.astype(jnp.bfloat16)
        out.append(p)
        x = x - p.astype(np.float32)
    return np.stack(out)


def _np_tables():
    r = np.arange(N)
    ang = ((r[:, None] * r[None, :]) % N).astype(np.float32) * np.float32(2.0 * math.pi / N)
    c = np.cos(ang.astype(np.float64)).astype(np.float32)
    s = np.sin(ang.astype(np.float64)).astype(np.float32)
    cs = np.stack([_np_split(c), _np_split(s)], 1)
    t1 = np.concatenate([c[:H + 1], -s[1:H]], 0)
    wgt = np.where((r == 0) | (r == H), 1.0, 2.0).astype(np.float32) / N
    t5 = np.concatenate([c[:, :H + 1] * wgt[:H + 1], -s[:, 1:H] * wgt[1:H]], 1)
    return cs, _np_split(t1), _np_split(t5)


def _split(x):
    h = x.astype(BF16)
    r = x - h.astype(F32)
    m = r.astype(BF16)
    return h, m, (r - m.astype(F32)).astype(BF16)


PAIRS = ((0, 0), (0, 1), (1, 0), (1, 1), (0, 2), (2, 0))


def _dot6(ls, rs):
    acc = None
    for i, j in PAIRS:
        d = jnp.dot(ls[i], rs[j], preferred_element_type=F32)
        acc = d if acc is None else acc + d
    return acc


def _k2(t_ref, v_ref, o_ref):
    re = jnp.swapaxes(v_ref[:H, :, :H], 0, 1)
    im = jnp.swapaxes(jnp.concatenate([v_ref[H:H + 1, :, :H], v_ref[1:H, :, H:]], 0), 0, 1)
    tab = [t_ref[p] for p in range(3)]
    outs = []
    for j in range(4):
        x = jnp.concatenate([
            jnp.concatenate([re[2 * j], re[2 * j + 1]], axis=1),
            jnp.concatenate([im[2 * j], im[2 * j + 1]], axis=1)], axis=0)
        acc = _dot6(tab, _split(x))
        outs += [acc[:, :H], acc[:, H:]]
    o_ref[...] = jnp.swapaxes(jnp.stack(outs), 0, 1)


def _k1(t1_ref, cs_ref, u_ref, g_ref, v_ref, us, xs, r1, y2, r2, r3, gv, w3, w3i, t4,
        usem, gsem, s1, q1, s2, q2, s3, q3, s4, q4, l4):
    a = lax.axis_index("a")
    b = lax.axis_index("b")
    ob = 1 - b

    def ucopy(j):
        return pltpu.make_async_copy(
            u_ref.at[:, pl.ds(pl.multiple_of(j * G, G), G), :], us.at[lax.rem(j, US)],
            usem.at[lax.rem(j, US)])

    gcopy = pltpu.make_async_copy(g_ref, gv, gsem)

    @pl.loop(0, US)
    def _(j):
        ucopy(j).start()

    barrier = pltpu.get_barrier_semaphore()
    for d in range(1, NA):
        pl.semaphore_signal(barrier, inc=1, device_id=(b, lax.rem(a + d, NA)), device_id_type=MESH)
    pl.semaphore_signal(barrier, inc=1, device_id=(ob, a), device_id_type=MESH)

    def rows(blk):
        return pl.ds(pl.multiple_of(blk * YA, YA), YA)

    own = pl.ds(pl.multiple_of(b * H, H), H)
    oth = pl.ds(pl.multiple_of(ob * H, H), H)

    def e1(k, to):
        return pltpu.make_async_remote_copy(
            src_ref=xs.at[to * KB + k], dst_ref=r1.at[k, rows(a)],
            send_sem=s1, recv_sem=q1.at[k], device_id=(b, to), device_id_type=MESH)

    def e1_group(k, j, to):
        return pltpu.make_async_remote_copy(
            src_ref=xs.at[to * KB + k, pl.ds(pl.multiple_of(j * G, G), G)],
            dst_ref=r1.at[k, pl.ds(pl.multiple_of(a * YA + j * G, G), G)],
            send_sem=s1, recv_sem=q1.at[k], device_id=(b, to), device_id_type=MESH)

    def e2(k):
        return pltpu.make_async_remote_copy(
            src_ref=y2.at[k, oth], dst_ref=r2.at[k],
            send_sem=s2, recv_sem=q2.at[k], device_id=(ob, a), device_id_type=MESH)

    def e3(k):
        return pltpu.make_async_remote_copy(
            src_ref=r2.at[k], dst_ref=r3.at[k],
            send_sem=s3, recv_sem=q3.at[k], device_id=(ob, a), device_id_type=MESH)

    def e4(k, to):
        return pltpu.make_async_remote_copy(
            src_ref=r1.at[k, rows(to)], dst_ref=v_ref.at[a * KB + k],
            send_sem=s4, recv_sem=q4, device_id=(b, to), device_id_type=MESH)

    def e4_own(k):
        return pltpu.make_async_copy(r1.at[k, rows(a)], v_ref.at[a * KB + k], l4)

    def wait_bytes(ref, sem):
        pltpu.make_async_copy(ref, ref, sem).wait()

    others = [lax.rem(a + d, NA) for d in (2, 1, 3)]

    @pl.loop(0, NG)
    def _(j):
        ucopy(j).wait()
        t = jnp.swapaxes(us[lax.rem(j, US)], 0, 1)
        tab = [t1_ref[p] for p in range(3)]
        res, ims = [], []
        for q in range(G // 2):
            x = jnp.concatenate([t[2 * q], t[2 * q + 1]], axis=1)
            acc = _dot6(tab, _split(x))
            res += [acc[:H, :H], acc[:H, H:]]
            ims += [acc[H:, :H], acc[H:, H:]]
        re = jnp.swapaxes(jnp.stack(res), 0, 1)
        im = jnp.swapaxes(jnp.stack(ims), 0, 1)
        z = jnp.zeros((1, G, H), F32)
        yr = pl.ds(pl.multiple_of(j * G, G), G)
        xs[:H, yr, :H] = re
        xs[0:1, yr, H:] = z
        xs[1:H, yr, H:] = im[1:]
        xs[H:H + 1, yr, :H] = im[0:1]
        xs[H:H + 1, yr, H:] = z
        xs[H + 1:, yr, :] = jnp.zeros((NA * KB - H - 1, G, N), F32)
        r1[:, pl.ds(pl.multiple_of(a * YA + j * G, G), G), :] = xs[pl.ds(a * KB, KB), yr, :]

        @pl.when(j + US < NG)
        def _():
            ucopy(j + US).start()

        @pl.when(j == 0)
        def _():
            pl.semaphore_wait(barrier, NA)

        for k in range(EARLY):
            for to in others:
                e1_group(k, j, to).start()

    @pl.loop(EARLY, KB)
    def _(k):
        for to in others:
            e1(k, to).start()

    gcopy.start()

    def tables():
        for p in range(3):
            for k, sl in ((0, own), (1, oth)):
                cr, sr = cs_ref[p, 0, sl, :], cs_ref[p, 1, sl, :]
                w3[p, k * N:k * N + H, :N] = cr
                w3[p, k * N:k * N + H, N:] = -sr
                w3[p, k * N + H:(k + 1) * N, :N] = sr
                w3[p, k * N + H:(k + 1) * N, N:] = cr
                cc = (cs_ref[p, 0, :, sl].astype(F32) * (1.0 / N)).astype(BF16)
                sc = (cs_ref[p, 1, :, sl].astype(F32) * (1.0 / N)).astype(BF16)
                w3i[p, :N, k * N:k * N + H] = cc
                w3i[p, :N, k * N + H:(k + 1) * N] = sc
                w3i[p, N:, k * N:k * N + H] = -sc
                w3i[p, N:, k * N + H:(k + 1) * N] = cc
                t4[p, :N, k * H:(k + 1) * H] = cc
                t4[p, N:, k * H:(k + 1) * H] = sc

    def stage2(k):
        wait_bytes(r1.at[k, pl.ds(0, (NA - 1) * YA)], q1.at[k])
        acc = _dot6([cs_ref[q].reshape(2 * N, N) for q in range(3)], _split(r1[k]))
        y2[k, :, :H] = acc[:N, :H] + acc[N:, H:]
        y2[k, :, H:] = acc[:N, H:] - acc[N:, :H]
        e2(k).start()

    def stage3(k):
        e2(k).wait_recv()
        x = _split(jnp.concatenate([y2[k, own, :], r2[k]], axis=1))
        z = _dot6(x, [w3[q] for q in range(3)])
        gk = gv[k]
        z = _split(jnp.concatenate([z[:, :N] * gk, z[:, N:] * gk], axis=1))
        z = _dot6(z, [w3i[q] for q in range(3)])
        y2[k, own, :] = z[:, :N]
        r2[k] = z[:, N:]
        e3(k).start()

    def stage4(k):
        e3(k).wait_recv()
        x = jnp.concatenate([y2[k, own, :], r3[k]], axis=0)
        acc = _dot6([t4[q] for q in range(3)], _split(x))
        r1[k, :, :H] = acc[:N, :H] - acc[N:, H:]
        r1[k, :, H:] = acc[:N, H:] + acc[N:, :H]
        for to in others:
            e4(k, to).start()
        e4_own(k).start()

    @pl.loop(0, KB + A2 + A3)
    def _(i):
        @pl.when(i < KB)
        def _():
            stage2(i)

        @pl.when(i == 0)
        def _():
            tables()
            gcopy.wait()

        @pl.when(jnp.logical_and(i >= A2, i < KB + A2))
        def _():
            stage3(i - A2)

        @pl.when(i >= A2 + A3)
        def _():
            stage4(i - A2 - A3)

    blocks = xs.at[pl.ds(0, (NA - 1) * KB)]
    wait_bytes(blocks, s1)
    wait_bytes(blocks, s4)
    wait_bytes(r2, s2)
    wait_bytes(r2, s3)
    wait_bytes(xs.at[pl.ds(0, KB)], l4)
    wait_bytes(blocks, q4)


def solution(mesh):
    cs_np, t1_np, t5_np = _np_tables()
    dma = pltpu.SemaphoreType.DMA

    def local(u, g):
        cs, t1, t5 = jnp.asarray(cs_np), jnp.asarray(t1_np), jnp.asarray(t5_np)
        full = pl.BlockSpec((3, N, N), lambda i: (0, 0, 0))
        params = pltpu.CompilerParams(vmem_limit_bytes=60 * 2**20)
        any_ = pl.BlockSpec(memory_space=pl.ANY)
        vmem = pl.BlockSpec(memory_space=pltpu.VMEM)
        v = pl.pallas_call(
            _k1, name="fwd_yz",
            in_specs=[vmem, vmem, any_, any_],
            out_specs=any_,
            out_shape=jax.ShapeDtypeStruct((NA * KB, YA, N), F32),
            scratch_shapes=[
                pltpu.VMEM((US, N, G, H), F32), pltpu.VMEM((NA * KB, YA, N), F32),
                pltpu.VMEM((KB, N, N), F32), pltpu.VMEM((KB, N, N), F32),
                pltpu.VMEM((KB, H, N), F32), pltpu.VMEM((KB, H, N), F32),
                pltpu.VMEM((KB, H, N), F32),
                pltpu.VMEM((3, 2 * N, 2 * N), BF16), pltpu.VMEM((3, 2 * N, 2 * N), BF16),
                pltpu.VMEM((3, 2 * N, N), BF16),
                dma((US,)), dma, dma, dma((KB,)), dma, dma((KB,)), dma, dma((KB,)), dma, dma, dma,
            ],
            compiler_params=pltpu.CompilerParams(
                collective_id=0, has_side_effects=True, vmem_limit_bytes=60 * 2**20),
        )(t1, cs, u, g)
        return pl.pallas_call(
            _k2, grid=(YA // 8,), name="inv_x",
            in_specs=[full, pl.BlockSpec((NA * KB, 8, N), lambda i: (0, i, 0))],
            out_specs=pl.BlockSpec((N, 8, H), lambda i: (0, i, 0)),
            out_shape=jax.ShapeDtypeStruct((N, YA, H), F32),
            compiler_params=params,
        )(t5, v)

    return jax.shard_map(local, mesh=mesh, in_specs=(P(None, "a", "b"), P("a", "b", None)),
                         out_specs=P(None, "a", "b"), check_vma=False)
```

time: 246 us -> 225 us (0.915)
  Pallas kernels: 245 us -> 224 us
    pallas_call x2 -> x1, Pallas kernels: 232 us -> 211 us  [local(): pl.pallas_call(_k1, name='fwd_yz', in_specs=[vmem, vmem, any_, any_], out...]
where the time goes in v2:
time: 225 us; the launch traced here: 224 us
  Pallas kernels  224 us (100%)
    pallas_call x1, Pallas kernels, local(): pl.pallas_call(_k1, name='fwd_yz', in_specs=[vmem, vmem, any_, any_], out...  211 us
    pallas_call x1, Pallas kernels, local(): pl.pallas_call(_k2, grid=(YA // 8,), name='inv_x', in_specs=[full, pl.Blo...  13.4 us

profile of v2, /device:TPU:0, one launch (start us, length us, event | category | flops | bytes accessed | tf_op | source)
XLA Modules:
  0.0 224.2 jit_solution(1907725457062666605)
XLA Ops:
  0.0 210.8 %fwd_yz.1.v_ref = f32[132,64,256]{2,1,0:T(8,128)} custom-call(bf16[3,256,256]{2,1,0:T(8,128)(2,1)} %constant.7.clone.t1_ref, bf16[3,2,256,256]{3,2,1,0:T(8,128)(2,1)} %constant.6.clone.cs_ref, f32[256,64,128]{2,1,0:T(8,128)} %u_ref.1, f32[33,128,256]{2,1,0:T(8,128)} %g_ref.1), custom_call_target="tpu_custom_call" | custom-call | tf_op jit(solution)/shard_map/fwd_yz/pallas_call | solution.py:270
  210.8 13.4 %inv_x.1 = f32[256,64,128]{2,1,0:T(8,128)} custom-call(bf16[3,256,256]{2,1,0:T(8,128)(2,1)} %constant.8.clone.t_ref, f32[132,64,256]{2,1,0:T(8,128)} %fwd_yz.1.v_ref), custom_call_target="tpu_custom_call" | custom-call | tf_op jit(solution)/shard_map/inv_x/pallas_call | solution.py:287

commit v3 on v2

--- a/solution.py
+++ b/solution.py
@@ -18,7 +18,10 @@
 G = 8
 NG = YA // G
 US = 4
+ALT = 2
 EARLY = 2
+MID = 20
+LATE = 30
 A2 = 2
 A3 = 2
 F32 = jnp.float32
@@ -81,7 +84,9 @@
 
 
 def _k1(t1_ref, cs_ref, u_ref, g_ref, v_ref, us, xs, r1, y2, r2, r3, gv, w3, w3i, t4,
-        usem, gsem, s1, q1, s2, q2, s3, q3, s4, q4, l4):
+        gp, za, zs, ya, fa, zb, vo, vx,
+        usem, gsem, s1, q1, s2, q2, s3, q3, s4, q4, l4,
+        gpsem, sg, qg, sa1, qa1, sa3, qa3, sa6, qa6, sa8, qa8):
     a = lax.axis_index("a")
     b = lax.axis_index("b")
     ob = 1 - b
@@ -107,6 +112,7 @@
 
     own = pl.ds(pl.multiple_of(b * H, H), H)
     oth = pl.ds(pl.multiple_of(ob * H, H), H)
+    own_first, own_last = own, oth
 
     def e1(k, to):
         return pltpu.make_async_remote_copy(
@@ -136,6 +142,37 @@
 
     def e4_own(k):
         return pltpu.make_async_copy(r1.at[k, rows(a)], v_ref.at[a * KB + k], l4)
+
+    gp_own = pltpu.make_async_copy(g_ref.at[b], gp.at[pl.ds(0, H)], gpsem)
+
+    def gp_other():
+        return pltpu.make_async_remote_copy(
+            src_ref=g_ref.at[ob], dst_ref=gp.at[pl.ds(H, H)],
+            send_sem=sg, recv_sem=qg, device_id=(ob, a), device_id_type=MESH)
+
+    def a1(n, j):
+        yr = pl.ds(pl.multiple_of(j * G, G), G)
+        return pltpu.make_async_remote_copy(
+            src_ref=xs.at[n * KB + ob, yr], dst_ref=za.at[n, yr],
+            send_sem=sa1, recv_sem=qa1, device_id=(ob, a), device_id_type=MESH)
+
+    def a3(to):
+        return pltpu.make_async_remote_copy(
+            src_ref=zs.at[to], dst_ref=ya.at[rows(a)],
+            send_sem=sa3, recv_sem=qa3, device_id=(b, to), device_id_type=MESH)
+
+    def a6(to):
+        return pltpu.make_async_remote_copy(
+            src_ref=ya.at[rows(to)], dst_ref=zb.at[a],
+            send_sem=sa6, recv_sem=qa6, device_id=(b, to), device_id_type=MESH)
+
+    def a8(n):
+        return pltpu.make_async_remote_copy(
+            src_ref=vx.at[n], dst_ref=v_ref.at[n * KB + b],
+            send_sem=sa8, recv_sem=qa8, device_id=(ob, a), device_id_type=MESH)
+
+    def a8_own(n):
+        return pltpu.make_async_copy(vo.at[n], v_ref.at[n * KB + b], l4)
 
     def wait_bytes(ref, sem):
         pltpu.make_async_copy(ref, ref, sem).wait()
@@ -172,17 +209,21 @@
         @pl.when(j == 0)
         def _():
             pl.semaphore_wait(barrier, NA)
-
-        for k in range(EARLY):
+            gp_other().start()
+
+        for k in range(ALT, ALT + EARLY):
             for to in others:
                 e1_group(k, j, to).start()
-
-    @pl.loop(EARLY, KB)
+        for n in range(NA):
+            a1(n, j).start()
+
+    @pl.loop(ALT + EARLY, KB)
     def _(k):
         for to in others:
             e1(k, to).start()
 
     gcopy.start()
+    gp_own.start()
 
     def tables():
         for p in range(3):
@@ -229,32 +270,89 @@
             e4(k, to).start()
         e4_own(k).start()
 
-    @pl.loop(0, KB + A2 + A3)
+    def alt_z():
+        wait_bytes(za, qa1)
+        x = jnp.concatenate([xs[n * KB + b] for n in range(NA)], axis=0)
+        x = jnp.concatenate([x, za[...].reshape(NA * YA, N)], axis=1)
+        zs[...] = _dot6(_split(x), [w3[q] for q in range(3)]).reshape(NA, YA, 2 * N)
+        for to in others:
+            a3(to).start()
+        ya[rows(a), :] = zs[a]
+
+    def alt_y():
+        wait_bytes(zs.at[pl.ds(0, NA - 1)], qa3)
+        wait_bytes(gp.at[pl.ds(H, H)], qg)
+        gp_own.wait()
+        for q in range(2):
+            x = jnp.concatenate([ya[:, q * H:(q + 1) * H], ya[:, N + q * H:N + (q + 1) * H]], axis=1)
+            acc = _dot6([cs_ref[p].reshape(2 * N, N) for p in range(3)], _split(x))
+            re = acc[:N, :H] + acc[N:, H:]
+            im = acc[:N, H:] - acc[N:, :H]
+            fa[own_first, :H], fa[own_first, H:] = re[:H], im[:H]
+            fa[own_last, :H], fa[own_last, H:] = re[H:], im[H:]
+            gq = gp[:, q * H:(q + 1) * H]
+            x = fa[...] * jnp.concatenate([gq, gq], axis=1)
+            acc = _dot6([t4[p] for p in range(3)], _split(x))
+            ya[:, q * H:(q + 1) * H] = acc[:N, :H] - acc[N:, H:]
+            ya[:, N + q * H:N + (q + 1) * H] = acc[:N, H:] + acc[N:, :H]
+        for to in others:
+            a6(to).start()
+        zb[a] = ya[rows(a), :]
+
+    def alt_zinv():
+        wait_bytes(zs.at[pl.ds(0, NA - 1)], qa6)
+        z = _dot6(_split(zb[...].reshape(NA * YA, 2 * N)), [w3i[q] for q in range(3)])
+        vo[...] = z[:, :N].reshape(NA, YA, N)
+        vx[...] = z[:, N:].reshape(NA, YA, N)
+        for n in range(NA):
+            a8_own(n).start()
+
+    @pl.loop(ALT, KB + A2 + A3)
     def _(i):
         @pl.when(i < KB)
         def _():
             stage2(i)
 
-        @pl.when(i == 0)
+        @pl.when(i == ALT)
         def _():
             tables()
             gcopy.wait()
-
-        @pl.when(jnp.logical_and(i >= A2, i < KB + A2))
+            alt_z()
+
+        @pl.when(jnp.logical_and(i >= ALT + A2, i < KB + A2))
         def _():
             stage3(i - A2)
 
-        @pl.when(i >= A2 + A3)
+        @pl.when(i == MID)
+        def _():
+            alt_y()
+
+        @pl.when(i == LATE)
+        def _():
+            alt_zinv()
+
+        @pl.when(i == KB + A2 - 1)
+        def _():
+            for n in range(NA):
+                a8(n).start()
+
+        @pl.when(i >= ALT + A2 + A3)
         def _():
             stage4(i - A2 - A3)
 
-    blocks = xs.at[pl.ds(0, (NA - 1) * KB)]
+    blocks = xs.at[pl.ds(0, (NA - 1) * (KB - ALT))]
     wait_bytes(blocks, s1)
     wait_bytes(blocks, s4)
-    wait_bytes(r2, s2)
-    wait_bytes(r2, s3)
-    wait_bytes(xs.at[pl.ds(0, KB)], l4)
+    wait_bytes(r2.at[pl.ds(0, KB - ALT)], s2)
+    wait_bytes(r2.at[pl.ds(0, KB - ALT)], s3)
+    wait_bytes(gp.at[pl.ds(0, H)], sg)
+    wait_bytes(za, sa1)
+    wait_bytes(zs.at[pl.ds(0, NA - 1)], sa3)
+    wait_bytes(zs.at[pl.ds(0, NA - 1)], sa6)
+    wait_bytes(za, sa8)
+    wait_bytes(xs.at[pl.ds(0, KB - ALT + NA)], l4)
     wait_bytes(blocks, q4)
+    wait_bytes(za, qa8)
 
 
 def solution(mesh):
@@ -279,7 +377,12 @@
                 pltpu.VMEM((KB, H, N), F32),
                 pltpu.VMEM((3, 2 * N, 2 * N), BF16), pltpu.VMEM((3, 2 * N, 2 * N), BF16),
                 pltpu.VMEM((3, 2 * N, N), BF16),
+                pltpu.VMEM((N, N), F32), pltpu.VMEM((NA, YA, N), F32),
+                pltpu.VMEM((NA, YA, 2 * N), F32), pltpu.VMEM((N, 2 * N), F32),
+                pltpu.VMEM((N, N), F32), pltpu.VMEM((NA, YA, 2 * N), F32),
+                pltpu.VMEM((NA, YA, N), F32), pltpu.VMEM((NA, YA, N), F32),
                 dma((US,)), dma, dma, dma((KB,)), dma, dma((KB,)), dma, dma((KB,)), dma, dma, dma,
+                dma, dma, dma, dma, dma, dma, dma, dma, dma, dma, dma,
             ],
             compiler_params=pltpu.CompilerParams(
                 collective_id=0, has_side_effects=True, vmem_limit_bytes=60 * 2**20),

time: 225 us -> 215 us (0.956)
  Pallas kernels: 224 us -> 215 us
    pallas_call x1, Pallas kernels: 211 us -> 201 us  [local(): pl.pallas_call(_k1, name='fwd_yz', in_specs=[vmem, vmem, any_, any_], out...]
where the time goes in v3:
time: 215 us
  Pallas kernels  215 us (100%)
    pallas_call x1, Pallas kernels, local(): pl.pallas_call(_k1, name='fwd_yz', in_specs=[vmem, vmem, any_, any_], out...  201 us
    pallas_call x1, Pallas kernels, local(): pl.pallas_call(_k2, grid=(YA // 8,), name='inv_x', in_specs=[full, pl.Blo...  13.4 us

profile of v3, /device:TPU:0, one launch (start us, length us, event | category | flops | bytes accessed | tf_op | source)
XLA Modules:
  0.0 214.9 jit_solution(4112808830430965298)
XLA Ops:
  0.0 201.5 %fwd_yz.1.v_ref = f32[132,64,256]{2,1,0:T(8,128)} custom-call(bf16[3,256,256]{2,1,0:T(8,128)(2,1)} %constant.7.clone.t1_ref, bf16[3,2,256,256]{3,2,1,0:T(8,128)(2,1)} %constant.6.clone.cs_ref, f32[256,64,128]{2,1,0:T(8,128)} %u_ref.1, f32[33,128,256]{2,1,0:T(8,128)} %g_ref.1), custom_call_target="tpu_custom_call" | custom-call | tf_op jit(solution)/shard_map/fwd_yz/pallas_call | solution.py:368
  201.5 13.4 %inv_x.1 = f32[256,64,128]{2,1,0:T(8,128)} custom-call(bf16[3,256,256]{2,1,0:T(8,128)(2,1)} %constant.8.clone.t_ref, f32[132,64,256]{2,1,0:T(8,128)} %fwd_yz.1.v_ref), custom_call_target="tpu_custom_call" | custom-call | tf_op jit(solution)/shard_map/inv_x/pallas_call | solution.py:390

commit v4 on v3

--- a/solution.py
+++ b/solution.py
@@ -22,6 +22,13 @@
 EARLY = 2
 MID = 20
 LATE = 30
+NTP = 10
+NM = KB - NTP
+MAIN = np.arange(ALT, ALT + NM)
+TAIL = np.concatenate([np.arange(ALT), np.arange(ALT + NM, KB)])
+NT = NA * NTP
+I5 = 31
+PG = 3
 A2 = 2
 A3 = 2
 F32 = jnp.float32
@@ -46,9 +53,19 @@
     s = np.sin(ang.astype(np.float64)).astype(np.float32)
     cs = np.stack([_np_split(c), _np_split(s)], 1)
     t1 = np.concatenate([c[:H + 1], -s[1:H]], 0)
-    wgt = np.where((r == 0) | (r == H), 1.0, 2.0).astype(np.float32) / N
-    t5 = np.concatenate([c[:, :H + 1] * wgt[:H + 1], -s[:, 1:H] * wgt[1:H]], 1)
-    return cs, _np_split(t1), _np_split(t5)
+    kx = np.arange(NA * KB)
+    wgt = np.where((kx == 0) | (kx == H), 1.0, 2.0) * (kx <= H) / N
+    kc = np.minimum(kx, N - 1)
+    cr = (c[:, kc] * wgt).astype(np.float32)
+    ci = (-s[:, kc] * wgt).astype(np.float32)
+    blk = kx.reshape(NA, KB)
+    main = blk[:, MAIN].ravel()
+    tail = blk[:, TAIL].ravel()
+    pad = np.zeros((N, H - main.size), np.float32)
+    t5m = np.concatenate([cr[:, main], pad, ci[:, main], pad], 1)
+    t5t = _np_split(np.concatenate([cr[:, tail], ci[:, tail]], 1))
+    t5t = np.concatenate([t5t[i] for i, _ in PAIRS], 1)
+    return cs, _np_split(t1), _np_split(t5m), t5t
 
 
 def _split(x):
@@ -69,24 +86,50 @@
     return acc
 
 
-def _k2(t_ref, v_ref, o_ref):
-    re = jnp.swapaxes(v_ref[:H, :, :H], 0, 1)
-    im = jnp.swapaxes(jnp.concatenate([v_ref[H:H + 1, :, :H], v_ref[1:H, :, H:]], 0), 0, 1)
-    tab = [t_ref[p] for p in range(3)]
-    outs = []
-    for j in range(4):
-        x = jnp.concatenate([
-            jnp.concatenate([re[2 * j], re[2 * j + 1]], axis=1),
-            jnp.concatenate([im[2 * j], im[2 * j + 1]], axis=1)], axis=0)
-        acc = _dot6(tab, _split(x))
-        outs += [acc[:, :H], acc[:, H:]]
-    o_ref[...] = jnp.swapaxes(jnp.stack(outs), 0, 1)
-
-
-def _k1(t1_ref, cs_ref, u_ref, g_ref, v_ref, us, xs, r1, y2, r2, r3, gv, w3, w3i, t4,
+def _k2(t_ref, w_ref, v_ref, o_ref, buf, vt, isem, vsem, osem):
+    def yr(j):
+        return pl.ds(pl.multiple_of(j * G, G), G)
+
+    def rd(j):
+        return pltpu.make_async_copy(w_ref.at[j], buf.at[j], isem.at[j])
+
+    def wr(j):
+        return pltpu.make_async_copy(buf.at[j], o_ref.at[:, yr(j), :], osem.at[j])
+
+    vcopy = pltpu.make_async_copy(v_ref, vt, vsem)
+    vcopy.start()
+
+    @pl.loop(0, NG)
+    def _(j):
+        rd(j).start()
+
+    vcopy.wait()
+
+    @pl.loop(0, NG)
+    def _(j):
+        t = jnp.swapaxes(vt[:, yr(j), :], 0, 1)
+        outs = []
+        for q in range(G // 2):
+            x = jnp.concatenate([
+                jnp.concatenate([t[2 * q][:, :H], t[2 * q + 1][:, :H]], axis=1),
+                jnp.concatenate([t[2 * q][:, H:], t[2 * q + 1][:, H:]], axis=1)], axis=0)
+            p = _split(x)
+            x = jnp.concatenate([p[k] for _, k in PAIRS], axis=0)
+            acc = jnp.dot(t_ref[...], x, preferred_element_type=F32)
+            outs += [acc[:, :H], acc[:, H:]]
+        rd(j).wait()
+        buf[j] += jnp.swapaxes(jnp.stack(outs), 0, 1)
+        wr(j).start()
+
+    @pl.loop(0, NG)
+    def _(j):
+        wr(j).wait()
+
+
+def _k1(t1_ref, t5_ref, cs_ref, u_ref, g_ref, w_ref, vt_ref, us, v4, xs, r1, y2, r2, r3, gv, w3, w3i, t4,
         gp, za, zs, ya, fa, zb, vo, vx,
         usem, gsem, s1, q1, s2, q2, s3, q3, s4, q4, l4,
-        gpsem, sg, qg, sa1, qa1, sa3, qa3, sa6, qa6, sa8, qa8):
+        gpsem, sg, qg, sa1, qa1, sa3, qa3, sa6, qa6, sa8, qa8, q4t, osem):
     a = lax.axis_index("a")
     b = lax.axis_index("b")
     ob = 1 - b
@@ -137,11 +180,16 @@
 
     def e4(k, to):
         return pltpu.make_async_remote_copy(
-            src_ref=r1.at[k, rows(to)], dst_ref=v_ref.at[a * KB + k],
+            src_ref=r1.at[k, rows(to)], dst_ref=v4.at[a * NM + k - ALT],
             send_sem=s4, recv_sem=q4, device_id=(b, to), device_id_type=MESH)
 
-    def e4_own(k):
-        return pltpu.make_async_copy(r1.at[k, rows(a)], v_ref.at[a * KB + k], l4)
+    def e4_tail(k, to):
+        return pltpu.make_async_remote_copy(
+            src_ref=r1.at[k, rows(to)], dst_ref=vt_ref.at[a * NTP + k - NM],
+            send_sem=s4, recv_sem=q4t, device_id=(b, to), device_id_type=MESH)
+
+    def e4_tail_own(k):
+        return pltpu.make_async_copy(r1.at[k, rows(a)], vt_ref.at[a * NTP + k - NM], l4)
 
     gp_own = pltpu.make_async_copy(g_ref.at[b], gp.at[pl.ds(0, H)], gpsem)
 
@@ -168,11 +216,11 @@
 
     def a8(n):
         return pltpu.make_async_remote_copy(
-            src_ref=vx.at[n], dst_ref=v_ref.at[n * KB + b],
+            src_ref=vx.at[n], dst_ref=vt_ref.at[n * NTP + b],
             send_sem=sa8, recv_sem=qa8, device_id=(ob, a), device_id_type=MESH)
 
     def a8_own(n):
-        return pltpu.make_async_copy(vo.at[n], v_ref.at[n * KB + b], l4)
+        return pltpu.make_async_copy(vo.at[n], vt_ref.at[n * NTP + b], l4)
 
     def wait_bytes(ref, sem):
         pltpu.make_async_copy(ref, ref, sem).wait()
@@ -266,9 +314,18 @@
         acc = _dot6([t4[q] for q in range(3)], _split(x))
         r1[k, :, :H] = acc[:N, :H] - acc[N:, H:]
         r1[k, :, H:] = acc[:N, H:] + acc[N:, :H]
-        for to in others:
-            e4(k, to).start()
-        e4_own(k).start()
+
+        @pl.when(k < ALT + NM)
+        def _():
+            for to in others:
+                e4(k, to).start()
+            v4[a * NM + k - ALT] = r1[k, rows(a), :]
+
+        @pl.when(k >= ALT + NM)
+        def _():
+            for to in others:
+                e4_tail(k, to).start()
+            e4_tail_own(k).start()
 
     def alt_z():
         wait_bytes(za, qa1)
@@ -307,6 +364,30 @@
         for n in range(NA):
             a8_own(n).start()
 
+    def wr(j):
+        return pltpu.make_async_copy(
+            us.at[lax.rem(j, US)], w_ref.at[j], osem.at[lax.rem(j, US)])
+
+    def inv_x(j):
+        @pl.when(j >= US)
+        def _():
+            wr(j - US).wait()
+
+        yr = pl.ds(pl.multiple_of(j * G, G), G)
+        z = jnp.zeros((H - NA * NM, G, H), F32)
+        re = jnp.swapaxes(jnp.concatenate([v4[:, yr, :H], z], axis=0), 0, 1)
+        im = jnp.swapaxes(jnp.concatenate([v4[:, yr, H:], z], axis=0), 0, 1)
+        tab = [t5_ref[p] for p in range(3)]
+        outs = []
+        for q in range(G // 2):
+            x = jnp.concatenate([
+                jnp.concatenate([re[2 * q], re[2 * q + 1]], axis=1),
+                jnp.concatenate([im[2 * q], im[2 * q + 1]], axis=1)], axis=0)
+            acc = _dot6(tab, _split(x))
+            outs += [acc[:, :H], acc[:, H:]]
+        us[lax.rem(j, US)] = jnp.swapaxes(jnp.stack(outs), 0, 1)
+        wr(j).start()
+
     @pl.loop(ALT, KB + A2 + A3)
     def _(i):
         @pl.when(i < KB)
@@ -339,6 +420,20 @@
         @pl.when(i >= ALT + A2 + A3)
         def _():
             stage4(i - A2 - A3)
+
+        @pl.when(i == I5)
+        def _():
+            wait_bytes(v4.at[pl.ds(0, (NA - 1) * NM)], q4)
+
+        @pl.when(i >= I5)
+        def _():
+            @pl.loop((i - I5) * PG, jnp.minimum((i - I5 + 1) * PG, NG))
+            def _(j):
+                inv_x(j)
+
+    @pl.loop(NG - US, NG)
+    def _(j):
+        wr(j).wait()
 
     blocks = xs.at[pl.ds(0, (NA - 1) * (KB - ALT))]
     wait_bytes(blocks, s1)
@@ -350,28 +445,27 @@
     wait_bytes(zs.at[pl.ds(0, NA - 1)], sa3)
     wait_bytes(zs.at[pl.ds(0, NA - 1)], sa6)
     wait_bytes(za, sa8)
-    wait_bytes(xs.at[pl.ds(0, KB - ALT + NA)], l4)
-    wait_bytes(blocks, q4)
+    wait_bytes(xs.at[pl.ds(0, NTP - ALT + NA)], l4)
+    wait_bytes(xs.at[pl.ds(0, (NTP - ALT) * (NA - 1))], q4t)
     wait_bytes(za, qa8)
 
 
 def solution(mesh):
-    cs_np, t1_np, t5_np = _np_tables()
+    cs_np, t1_np, t5m_np, t5t_np = _np_tables()
     dma = pltpu.SemaphoreType.DMA
 
     def local(u, g):
-        cs, t1, t5 = jnp.asarray(cs_np), jnp.asarray(t1_np), jnp.asarray(t5_np)
-        full = pl.BlockSpec((3, N, N), lambda i: (0, 0, 0))
-        params = pltpu.CompilerParams(vmem_limit_bytes=60 * 2**20)
+        cs, t1, t5m, t5t = (jnp.asarray(t) for t in (cs_np, t1_np, t5m_np, t5t_np))
         any_ = pl.BlockSpec(memory_space=pl.ANY)
         vmem = pl.BlockSpec(memory_space=pltpu.VMEM)
-        v = pl.pallas_call(
+        w, vt = pl.pallas_call(
             _k1, name="fwd_yz",
-            in_specs=[vmem, vmem, any_, any_],
-            out_specs=any_,
-            out_shape=jax.ShapeDtypeStruct((NA * KB, YA, N), F32),
+            in_specs=[vmem, vmem, vmem, any_, any_],
+            out_specs=[any_, any_],
+            out_shape=[jax.ShapeDtypeStruct((NG, N, G, H), F32), jax.ShapeDtypeStruct((NT, YA, N), F32)],
             scratch_shapes=[
-                pltpu.VMEM((US, N, G, H), F32), pltpu.VMEM((NA * KB, YA, N), F32),
+                pltpu.VMEM((US, N, G, H), F32), pltpu.VMEM((NA * NM, YA, N), F32),
+                pltpu.VMEM((NA * KB, YA, N), F32),
                 pltpu.VMEM((KB, N, N), F32), pltpu.VMEM((KB, N, N), F32),
                 pltpu.VMEM((KB, H, N), F32), pltpu.VMEM((KB, H, N), F32),
                 pltpu.VMEM((KB, H, N), F32),
@@ -382,18 +476,20 @@
                 pltpu.VMEM((N, N), F32), pltpu.VMEM((NA, YA, 2 * N), F32),
                 pltpu.VMEM((NA, YA, N), F32), pltpu.VMEM((NA, YA, N), F32),
                 dma((US,)), dma, dma, dma((KB,)), dma, dma((KB,)), dma, dma((KB,)), dma, dma, dma,
-                dma, dma, dma, dma, dma, dma, dma, dma, dma, dma, dma,
+                dma, dma, dma, dma, dma, dma, dma, dma, dma, dma, dma, dma, dma((US,)),
             ],
             compiler_params=pltpu.CompilerParams(
-                collective_id=0, has_side_effects=True, vmem_limit_bytes=60 * 2**20),
-        )(t1, cs, u, g)
+                collective_id=0, has_side_effects=True, vmem_limit_bytes=63 * 2**20),
+        )(t1, t5m, cs, u, g)
         return pl.pallas_call(
-            _k2, grid=(YA // 8,), name="inv_x",
-            in_specs=[full, pl.BlockSpec((NA * KB, 8, N), lambda i: (0, i, 0))],
-            out_specs=pl.BlockSpec((N, 8, H), lambda i: (0, i, 0)),
+            _k2, name="inv_x",
+            in_specs=[vmem, any_, any_], out_specs=any_,
             out_shape=jax.ShapeDtypeStruct((N, YA, H), F32),
-            compiler_params=params,
-        )(t5, v)
+            scratch_shapes=[
+                pltpu.VMEM((NG, N, G, H), F32), pltpu.VMEM((NT, YA, N), F32),
+                dma((NG,)), dma, dma((NG,))],
+            compiler_params=pltpu.CompilerParams(vmem_limit_bytes=60 * 2**20),
+        )(t5t, w, vt)
 
     return jax.shard_map(local, mesh=mesh, in_specs=(P(None, "a", "b"), P("a", "b", None)),
                          out_specs=P(None, "a", "b"), check_vma=False)

time: 215 us -> 211 us (0.981)
  Pallas kernels: 215 us -> 211 us
    pallas_call x2, Pallas kernels: 215 us -> 211 us  [the longest x1 201 us: local(): pl.pallas_call(_k1, name='fwd_yz', in_specs=[vmem, vmem, vmem, any_, any_...]
where the time goes in v4:
time: 211 us
  Pallas kernels  211 us (100%)
    pallas_call x1, Pallas kernels, local(): pl.pallas_call(_k1, name='fwd_yz', in_specs=[vmem, vmem, vmem, any_, any_...  201 us
    pallas_call x1, Pallas kernels, local(): pl.pallas_call(_k2, name='inv_x', in_specs=[vmem, any_, any_], out_specs=...  9.44 us

profile of v4, /device:TPU:0, one launch (start us, length us, event | category | flops | bytes accessed | tf_op | source)
XLA Modules:
  0.0 210.8 jit_solution(5173901252041332344)
XLA Ops:
  0.0 201.3 %fwd_yz.1 = (f32[8,256,8,128]{3,2,1,0:T(8,128)}, f32[40,64,256]{2,1,0:T(8,128)}) custom-call(bf16[3,256,256]{2,1,0:T(8,128)(2,1)} %constant.9.clone.t1_ref, bf16[3,256,256]{2,1,0:T(8,128)(2,1)} %constant.10.clone.t5_ref, bf16[3,2,256,256]{3,2,1,0:T(8,128)(2,1)} %constant.8.clone.cs_ref, f32[256,64,128]{2,1,0:T(8,128)} %u_ref.1, f32[33,128,256]{2,1,0:T(8,128)} %g_ref.1), custom_call_target="tpu_custom_call" | custom-call | tf_op jit(solution)/shard_map/fwd_yz/pallas_call | solution.py:461
  201.3 9.4 %inv_x.1 = f32[256,64,128]{2,1,0:T(8,128)} custom-call(bf16[256,480]{1,0:T(8,128)(2,1)} %constant.11.clone.t_ref, f32[8,256,8,128]{3,2,1,0:T(8,128)} %get-tuple-element.7.w_ref, f32[40,64,256]{2,1,0:T(8,128)} %get-tuple-element.8.v_ref), custom_call_target="tpu_custom_call" | custom-call | tf_op jit(solution)/shard_map/inv_x/pallas_call | solution.py:484

commit v5 on v4

--- a/solution.py
+++ b/solution.py
@@ -17,7 +17,8 @@
 YA = 64
 G = 8
 NG = YA // G
-US = 4
+VM = 52
+US = 3
 ALT = 2
 EARLY = 2
 MID = 20
@@ -27,6 +28,8 @@
 MAIN = np.arange(ALT, ALT + NM)
 TAIL = np.concatenate([np.arange(ALT), np.arange(ALT + NM, KB)])
 NT = NA * NTP
+NP = KB - ALT
+GS = 6
 I5 = 31
 PG = 3
 A2 = 2
@@ -86,28 +89,16 @@
     return acc
 
 
-def _k2(t_ref, w_ref, v_ref, o_ref, buf, vt, isem, vsem, osem):
+def _k2(t_ref, w_ref, v_ref, o_ref, buf, osem):
     def yr(j):
         return pl.ds(pl.multiple_of(j * G, G), G)
 
-    def rd(j):
-        return pltpu.make_async_copy(w_ref.at[j], buf.at[j], isem.at[j])
-
     def wr(j):
         return pltpu.make_async_copy(buf.at[j], o_ref.at[:, yr(j), :], osem.at[j])
 
-    vcopy = pltpu.make_async_copy(v_ref, vt, vsem)
-    vcopy.start()
-
     @pl.loop(0, NG)
     def _(j):
-        rd(j).start()
-
-    vcopy.wait()
-
-    @pl.loop(0, NG)
-    def _(j):
-        t = jnp.swapaxes(vt[:, yr(j), :], 0, 1)
+        t = jnp.swapaxes(v_ref[:, yr(j), :], 0, 1)
         outs = []
         for q in range(G // 2):
             x = jnp.concatenate([
@@ -117,8 +108,7 @@
             x = jnp.concatenate([p[k] for _, k in PAIRS], axis=0)
             acc = jnp.dot(t_ref[...], x, preferred_element_type=F32)
             outs += [acc[:, :H], acc[:, H:]]
-        rd(j).wait()
-        buf[j] += jnp.swapaxes(jnp.stack(outs), 0, 1)
+        buf[j] = w_ref[j] + jnp.swapaxes(jnp.stack(outs), 0, 1)
         wr(j).start()
 
     @pl.loop(0, NG)
@@ -127,9 +117,9 @@
 
 
 def _k1(t1_ref, t5_ref, cs_ref, u_ref, g_ref, w_ref, vt_ref, us, v4, xs, r1, y2, r2, r3, gv, w3, w3i, t4,
-        gp, za, zs, ya, fa, zb, vo, vx,
-        usem, gsem, s1, q1, s2, q2, s3, q3, s4, q4, l4,
-        gpsem, sg, qg, sa1, qa1, sa3, qa3, sa6, qa6, sa8, qa8, q4t, osem):
+        gp, za, zs, ya, fa, zb, vx,
+        usem, gsem, s1, q1, s2, q2, s3, q3, s4, q4,
+        gpsem, sg, qg, sa1, qa1, sa3, qa3, sa6, qa6, sa8, qa8, q4t):
     a = lax.axis_index("a")
     b = lax.axis_index("b")
     ob = 1 - b
@@ -139,7 +129,8 @@
             u_ref.at[:, pl.ds(pl.multiple_of(j * G, G), G), :], us.at[lax.rem(j, US)],
             usem.at[lax.rem(j, US)])
 
-    gcopy = pltpu.make_async_copy(g_ref, gv, gsem)
+    def gcopy(k):
+        return pltpu.make_async_copy(g_ref.at[k], gv.at[lax.rem(k, GS)], gsem.at[lax.rem(k, GS)])
 
     @pl.loop(0, US)
     def _(j):
@@ -159,37 +150,34 @@
 
     def e1(k, to):
         return pltpu.make_async_remote_copy(
-            src_ref=xs.at[to * KB + k], dst_ref=r1.at[k, rows(a)],
+            src_ref=xs.at[to * KB + k], dst_ref=r1.at[k - ALT, rows(a)],
             send_sem=s1, recv_sem=q1.at[k], device_id=(b, to), device_id_type=MESH)
 
     def e1_group(k, j, to):
         return pltpu.make_async_remote_copy(
             src_ref=xs.at[to * KB + k, pl.ds(pl.multiple_of(j * G, G), G)],
-            dst_ref=r1.at[k, pl.ds(pl.multiple_of(a * YA + j * G, G), G)],
+            dst_ref=r1.at[k - ALT, pl.ds(pl.multiple_of(a * YA + j * G, G), G)],
             send_sem=s1, recv_sem=q1.at[k], device_id=(b, to), device_id_type=MESH)
 
     def e2(k):
         return pltpu.make_async_remote_copy(
-            src_ref=y2.at[k, oth], dst_ref=r2.at[k],
+            src_ref=y2.at[k - ALT, oth], dst_ref=r2.at[k - ALT],
             send_sem=s2, recv_sem=q2.at[k], device_id=(ob, a), device_id_type=MESH)
 
     def e3(k):
         return pltpu.make_async_remote_copy(
-            src_ref=r2.at[k], dst_ref=r3.at[k],
+            src_ref=r2.at[k - ALT], dst_ref=r3.at[k - ALT],
             send_sem=s3, recv_sem=q3.at[k], device_id=(ob, a), device_id_type=MESH)
 
     def e4(k, to):
         return pltpu.make_async_remote_copy(
-            src_ref=r1.at[k, rows(to)], dst_ref=v4.at[a * NM + k - ALT],
+            src_ref=r1.at[k - ALT, rows(to)], dst_ref=v4.at[a * NM + k - ALT],
             send_sem=s4, recv_sem=q4, device_id=(b, to), device_id_type=MESH)
 
     def e4_tail(k, to):
         return pltpu.make_async_remote_copy(
-            src_ref=r1.at[k, rows(to)], dst_ref=vt_ref.at[a * NTP + k - NM],
+            src_ref=r1.at[k - ALT, rows(to)], dst_ref=vt_ref.at[a * NTP + k - NM],
             send_sem=s4, recv_sem=q4t, device_id=(b, to), device_id_type=MESH)
-
-    def e4_tail_own(k):
-        return pltpu.make_async_copy(r1.at[k, rows(a)], vt_ref.at[a * NTP + k - NM], l4)
 
     gp_own = pltpu.make_async_copy(g_ref.at[b], gp.at[pl.ds(0, H)], gpsem)
 
@@ -218,9 +206,6 @@
         return pltpu.make_async_remote_copy(
             src_ref=vx.at[n], dst_ref=vt_ref.at[n * NTP + b],
             send_sem=sa8, recv_sem=qa8, device_id=(ob, a), device_id_type=MESH)
-
-    def a8_own(n):
-        return pltpu.make_async_copy(vo.at[n], vt_ref.at[n * NTP + b], l4)
 
     def wait_bytes(ref, sem):
         pltpu.make_async_copy(ref, ref, sem).wait()
@@ -248,7 +233,7 @@
         xs[H:H + 1, yr, :H] = im[0:1]
         xs[H:H + 1, yr, H:] = z
         xs[H + 1:, yr, :] = jnp.zeros((NA * KB - H - 1, G, N), F32)
-        r1[:, pl.ds(pl.multiple_of(a * YA + j * G, G), G), :] = xs[pl.ds(a * KB, KB), yr, :]
+        r1[:, pl.ds(pl.multiple_of(a * YA + j * G, G), G), :] = xs[pl.ds(a * KB + ALT, NP), yr, :]
 
         @pl.when(j + US < NG)
         def _():
@@ -270,7 +255,10 @@
         for to in others:
             e1(k, to).start()
 
-    gcopy.start()
+    @pl.loop(ALT, ALT + GS)
+    def _(k):
+        gcopy(k).start()
+
     gp_own.start()
 
     def tables():
@@ -291,41 +279,46 @@
                 t4[p, N:, k * H:(k + 1) * H] = sc
 
     def stage2(k):
-        wait_bytes(r1.at[k, pl.ds(0, (NA - 1) * YA)], q1.at[k])
-        acc = _dot6([cs_ref[q].reshape(2 * N, N) for q in range(3)], _split(r1[k]))
-        y2[k, :, :H] = acc[:N, :H] + acc[N:, H:]
-        y2[k, :, H:] = acc[:N, H:] - acc[N:, :H]
+        wait_bytes(r1.at[k - ALT, pl.ds(0, (NA - 1) * YA)], q1.at[k])
+        acc = _dot6([cs_ref[q].reshape(2 * N, N) for q in range(3)], _split(r1[k - ALT]))
+        y2[k - ALT, :, :H] = acc[:N, :H] + acc[N:, H:]
+        y2[k - ALT, :, H:] = acc[:N, H:] - acc[N:, :H]
         e2(k).start()
 
     def stage3(k):
         e2(k).wait_recv()
-        x = _split(jnp.concatenate([y2[k, own, :], r2[k]], axis=1))
+        x = _split(jnp.concatenate([y2[k - ALT, own, :], r2[k - ALT]], axis=1))
         z = _dot6(x, [w3[q] for q in range(3)])
-        gk = gv[k]
+        gcopy(k).wait()
+        gk = gv[lax.rem(k, GS)]
         z = _split(jnp.concatenate([z[:, :N] * gk, z[:, N:] * gk], axis=1))
         z = _dot6(z, [w3i[q] for q in range(3)])
-        y2[k, own, :] = z[:, :N]
-        r2[k] = z[:, N:]
+        y2[k - ALT, own, :] = z[:, :N]
+        r2[k - ALT] = z[:, N:]
         e3(k).start()
+
+        @pl.when(k + GS < KB)
+        def _():
+            gcopy(k + GS).start()
 
     def stage4(k):
         e3(k).wait_recv()
-        x = jnp.concatenate([y2[k, own, :], r3[k]], axis=0)
+        x = jnp.concatenate([y2[k - ALT, own, :], r3[k - ALT]], axis=0)
         acc = _dot6([t4[q] for q in range(3)], _split(x))
-        r1[k, :, :H] = acc[:N, :H] - acc[N:, H:]
-        r1[k, :, H:] = acc[:N, H:] + acc[N:, :H]
+        r1[k - ALT, :, :H] = acc[:N, :H] - acc[N:, H:]
+        r1[k - ALT, :, H:] = acc[:N, H:] + acc[N:, :H]
 
         @pl.when(k < ALT + NM)
         def _():
             for to in others:
                 e4(k, to).start()
-            v4[a * NM + k - ALT] = r1[k, rows(a), :]
+            v4[a * NM + k - ALT] = r1[k - ALT, rows(a), :]
 
         @pl.when(k >= ALT + NM)
         def _():
             for to in others:
                 e4_tail(k, to).start()
-            e4_tail_own(k).start()
+            vt_ref[a * NTP + k - NM] = r1[k - ALT, rows(a), :]
 
     def alt_z():
         wait_bytes(za, qa1)
@@ -359,20 +352,11 @@
     def alt_zinv():
         wait_bytes(zs.at[pl.ds(0, NA - 1)], qa6)
         z = _dot6(_split(zb[...].reshape(NA * YA, 2 * N)), [w3i[q] for q in range(3)])
-        vo[...] = z[:, :N].reshape(NA, YA, N)
         vx[...] = z[:, N:].reshape(NA, YA, N)
         for n in range(NA):
-            a8_own(n).start()
-
-    def wr(j):
-        return pltpu.make_async_copy(
-            us.at[lax.rem(j, US)], w_ref.at[j], osem.at[lax.rem(j, US)])
+            vt_ref[n * NTP + b] = z[n * YA:(n + 1) * YA, :N]
 
     def inv_x(j):
-        @pl.when(j >= US)
-        def _():
-            wr(j - US).wait()
-
         yr = pl.ds(pl.multiple_of(j * G, G), G)
         z = jnp.zeros((H - NA * NM, G, H), F32)
         re = jnp.swapaxes(jnp.concatenate([v4[:, yr, :H], z], axis=0), 0, 1)
@@ -385,8 +369,7 @@
                 jnp.concatenate([im[2 * q], im[2 * q + 1]], axis=1)], axis=0)
             acc = _dot6(tab, _split(x))
             outs += [acc[:, :H], acc[:, H:]]
-        us[lax.rem(j, US)] = jnp.swapaxes(jnp.stack(outs), 0, 1)
-        wr(j).start()
+        w_ref[j] = jnp.swapaxes(jnp.stack(outs), 0, 1)
 
     @pl.loop(ALT, KB + A2 + A3)
     def _(i):
@@ -397,7 +380,6 @@
         @pl.when(i == ALT)
         def _():
             tables()
-            gcopy.wait()
             alt_z()
 
         @pl.when(jnp.logical_and(i >= ALT + A2, i < KB + A2))
@@ -431,21 +413,16 @@
             def _(j):
                 inv_x(j)
 
-    @pl.loop(NG - US, NG)
-    def _(j):
-        wr(j).wait()
-
     blocks = xs.at[pl.ds(0, (NA - 1) * (KB - ALT))]
     wait_bytes(blocks, s1)
     wait_bytes(blocks, s4)
-    wait_bytes(r2.at[pl.ds(0, KB - ALT)], s2)
-    wait_bytes(r2.at[pl.ds(0, KB - ALT)], s3)
+    wait_bytes(r2, s2)
+    wait_bytes(r2, s3)
     wait_bytes(gp.at[pl.ds(0, H)], sg)
     wait_bytes(za, sa1)
     wait_bytes(zs.at[pl.ds(0, NA - 1)], sa3)
     wait_bytes(zs.at[pl.ds(0, NA - 1)], sa6)
     wait_bytes(za, sa8)
-    wait_bytes(xs.at[pl.ds(0, NTP - ALT + NA)], l4)
     wait_bytes(xs.at[pl.ds(0, (NTP - ALT) * (NA - 1))], q4t)
     wait_bytes(za, qa8)
 
@@ -461,34 +438,33 @@
         w, vt = pl.pallas_call(
             _k1, name="fwd_yz",
             in_specs=[vmem, vmem, vmem, any_, any_],
-            out_specs=[any_, any_],
-            out_shape=[jax.ShapeDtypeStruct((NG, N, G, H), F32), jax.ShapeDtypeStruct((NT, YA, N), F32)],
+            out_specs=[vmem, vmem],
+            out_shape=[pltpu.VMEM((NG, N, G, H), F32), pltpu.VMEM((NT, YA, N), F32)],
             scratch_shapes=[
                 pltpu.VMEM((US, N, G, H), F32), pltpu.VMEM((NA * NM, YA, N), F32),
                 pltpu.VMEM((NA * KB, YA, N), F32),
-                pltpu.VMEM((KB, N, N), F32), pltpu.VMEM((KB, N, N), F32),
-                pltpu.VMEM((KB, H, N), F32), pltpu.VMEM((KB, H, N), F32),
-                pltpu.VMEM((KB, H, N), F32),
+                pltpu.VMEM((NP, N, N), F32), pltpu.VMEM((NP, N, N), F32),
+                pltpu.VMEM((NP, H, N), F32), pltpu.VMEM((NP, H, N), F32),
+                pltpu.VMEM((GS, H, N), F32),
                 pltpu.VMEM((3, 2 * N, 2 * N), BF16), pltpu.VMEM((3, 2 * N, 2 * N), BF16),
                 pltpu.VMEM((3, 2 * N, N), BF16),
                 pltpu.VMEM((N, N), F32), pltpu.VMEM((NA, YA, N), F32),
                 pltpu.VMEM((NA, YA, 2 * N), F32), pltpu.VMEM((N, 2 * N), F32),
                 pltpu.VMEM((N, N), F32), pltpu.VMEM((NA, YA, 2 * N), F32),
-                pltpu.VMEM((NA, YA, N), F32), pltpu.VMEM((NA, YA, N), F32),
-                dma((US,)), dma, dma, dma((KB,)), dma, dma((KB,)), dma, dma((KB,)), dma, dma, dma,
-                dma, dma, dma, dma, dma, dma, dma, dma, dma, dma, dma, dma, dma((US,)),
+                pltpu.VMEM((NA, YA, N), F32),
+                dma((US,)), dma((GS,)), dma, dma((KB,)), dma, dma((KB,)), dma, dma((KB,)), dma, dma,
+                dma, dma, dma, dma, dma, dma, dma, dma, dma, dma, dma, dma,
             ],
             compiler_params=pltpu.CompilerParams(
-                collective_id=0, has_side_effects=True, vmem_limit_bytes=63 * 2**20),
+                collective_id=0, has_side_effects=True, vmem_limit_bytes=VM * 2**20),
         )(t1, t5m, cs, u, g)
         return pl.pallas_call(
             _k2, name="inv_x",
-            in_specs=[vmem, any_, any_], out_specs=any_,
+            in_specs=[vmem, vmem, vmem], out_specs=any_,
             out_shape=jax.ShapeDtypeStruct((N, YA, H), F32),
             scratch_shapes=[
-                pltpu.VMEM((NG, N, G, H), F32), pltpu.VMEM((NT, YA, N), F32),
-                dma((NG,)), dma, dma((NG,))],
-            compiler_params=pltpu.CompilerParams(vmem_limit_bytes=60 * 2**20),
+                pltpu.VMEM((NG, N, G, H), F32), dma((NG,))],
+            compiler_params=pltpu.CompilerParams(vmem_limit_bytes=30 * 2**20),
         )(t5t, w, vt)
 
     return jax.shard_map(local, mesh=mesh, in_specs=(P(None, "a", "b"), P("a", "b", None)),

time: 211 us -> 207 us (0.981)
  Pallas kernels: 211 us -> 207 us
    pallas_call x1, Pallas kernels: 9.44 us -> 5.72 us  [local(): pl.pallas_call(_k2, name='inv_x', in_specs=[vmem, vmem, vmem], out_specs=...]
where the time goes in v5:
time: 207 us
  Pallas kernels  207 us (100%)
    pallas_call x1, Pallas kernels, local(): pl.pallas_call(_k1, name='fwd_yz', in_specs=[vmem, vmem, vmem, any_, any_...  201 us
    pallas_call x1, Pallas kernels, local(): pl.pallas_call(_k2, name='inv_x', in_specs=[vmem, vmem, vmem], out_specs=...  5.72 us

profile of v5, /device:TPU:0, one launch (start us, length us, event | category | flops | bytes accessed | tf_op | source)
XLA Modules:
  0.0 207.1 jit_solution(4303144129277756176)
XLA Ops:
  0.0 0.0 copy-start
  0.0 201.3 %fwd_yz.1 = (f32[8,256,8,128]{3,2,1,0:T(8,128)S(1)}, f32[40,64,256]{2,1,0:T(8,128)S(1)}) custom-call(bf16[3,256,256]{2,1,0:T(8,128)(2,1)} %constant.9.clone.t1_ref, bf16[3,256,256]{2,1,0:T(8,128)(2,1)} %constant.10.clone.t5_ref, bf16[3,2,256,256]{3,2,1,0:T(8,128)(2,1)} %constant.8.clone.cs_ref, f32[256,64,128]{2,1,0:T(8,128)} %u_ref.1, f32[33,128,256]{2,1,0:T(8,128)} %g_ref.1), custom_call_target="tpu_custom_call" | custom-call | tf_op jit(solution)/shard_map/fwd_yz/pallas_call | solution.py:438
  201.3 0.0 copy-done
  201.3 5.7 %inv_x.1 = f32[256,64,128]{2,1,0:T(8,128)} custom-call(bf16[256,480]{1,0:T(8,128)(2,1)S(1)} %copy-done, f32[8,256,8,128]{3,2,1,0:T(8,128)S(1)} %get-tuple-element.7.w_ref, f32[40,64,256]{2,1,0:T(8,128)S(1)} %get-tuple-element.8.v_ref), custom_call_target="tpu_custom_call" | custom-call | tf_op jit(solution)/shard_map/inv_x/pallas_call | solution.py:461
Async XLA Ops:
  0.0 201.3 %copy-start = (bf16[256,480]{1,0:T(8,128)(2,1)S(1)}, bf16[256,480]{1,0:T(8,128)(2,1)}, u32[]{:S(2)}) copy-start(bf16[256,480]{1,0:T(8,128)(2,1)} %constant.11.clone.t_ref) | copy-start | bytes 737284

commit v6 on v5

--- a/solution.py
+++ b/solution.py
@@ -28,6 +28,7 @@
 MAIN = np.arange(ALT, ALT + NM)
 TAIL = np.concatenate([np.arange(ALT), np.arange(ALT + NM, KB)])
 NT = NA * NTP
+REG = KB - 2
 NP = KB - ALT
 GS = 6
 I5 = 31
@@ -57,11 +58,13 @@
     cs = np.stack([_np_split(c), _np_split(s)], 1)
     t1 = np.concatenate([c[:H + 1], -s[1:H]], 0)
     kx = np.arange(NA * KB)
+    kx[3 * KB + REG - 1] = 2 * KB - 1
+    kx[[2 * KB - 1, 4 * KB - 2, 4 * KB - 1]] = NA * KB
     wgt = np.where((kx == 0) | (kx == H), 1.0, 2.0) * (kx <= H) / N
     kc = np.minimum(kx, N - 1)
     cr = (c[:, kc] * wgt).astype(np.float32)
     ci = (-s[:, kc] * wgt).astype(np.float32)
-    blk = kx.reshape(NA, KB)
+    blk = np.arange(NA * KB).reshape(NA, KB)
     main = blk[:, MAIN].ravel()
     tail = blk[:, TAIL].ravel()
     pad = np.zeros((N, H - main.size), np.float32)
@@ -116,10 +119,11 @@
         wr(j).wait()
 
 
-def _k1(t1_ref, t5_ref, cs_ref, u_ref, g_ref, w_ref, vt_ref, us, v4, xs, r1, y2, r2, r3, gv, w3, w3i, t4,
+def _k1(t1_ref, t5_hbm, cs_hbm, u_ref, g_ref, w_ref, vt_ref, t5_ref, cs_ref, gx, us, v4, xs, r1, y2, r2, r3, gv, w3, w3i, t4,
         gp, za, zs, ya, fa, zb, vx,
         usem, gsem, s1, q1, s2, q2, s3, q3, s4, q4,
-        gpsem, sg, qg, sa1, qa1, sa3, qa3, sa6, qa6, sa8, qa8, q4t):
+        gpsem, sg, qg, sa1, qa1, sa3, qa3, sa6, qa6, sa8, qa8, q4t,
+        tsem, sgx, qgx):
     a = lax.axis_index("a")
     b = lax.axis_index("b")
     ob = 1 - b
@@ -132,9 +136,18 @@
     def gcopy(k):
         return pltpu.make_async_copy(g_ref.at[k], gv.at[lax.rem(k, GS)], gsem.at[lax.rem(k, GS)])
 
+    nk = KB - lax.rem(a, 2) * (1 + a // 3)
+
     @pl.loop(0, US)
     def _(j):
         ucopy(j).start()
+
+    cscopy = pltpu.make_async_copy(cs_hbm, cs_ref, tsem.at[0])
+    t5copy = pltpu.make_async_copy(t5_hbm, t5_ref, tsem.at[1])
+    cscopy.start()
+    t5copy.start()
+    for n in (2 * NTP - 1, 4 * NTP - 2, 4 * NTP - 1):
+        vt_ref[n] = jnp.zeros((YA, N), F32)
 
     barrier = pltpu.get_barrier_semaphore()
     for d in range(1, NA):
@@ -146,38 +159,51 @@
 
     own = pl.ds(pl.multiple_of(b * H, H), H)
     oth = pl.ds(pl.multiple_of(ob * H, H), H)
+
+    def cls(k):
+        return jnp.maximum(k - (REG - 1), 0)
+
+    def used(blk, k):
+        return lax.rem(blk, 2) * (1 + blk // 3) < KB - k
+
     own_first, own_last = own, oth
 
-    def e1(k, to):
-        return pltpu.make_async_remote_copy(
-            src_ref=xs.at[to * KB + k], dst_ref=r1.at[k - ALT, rows(a)],
-            send_sem=s1, recv_sem=q1.at[k], device_id=(b, to), device_id_type=MESH)
+    def home(blk, k):
+        if isinstance(k, int) and k == REG - 1:
+            return blk * KB + k - (blk // 3) * (2 * KB - 2)
+        return blk * KB + k
+
+    def e1(k, to, sem=0):
+        return pltpu.make_async_remote_copy(
+            src_ref=xs.at[home(to, k)],
+            dst_ref=r1.at[k - ALT, rows(a)],
+            send_sem=s1.at[sem], recv_sem=q1.at[k], device_id=(b, to), device_id_type=MESH)
 
     def e1_group(k, j, to):
         return pltpu.make_async_remote_copy(
             src_ref=xs.at[to * KB + k, pl.ds(pl.multiple_of(j * G, G), G)],
             dst_ref=r1.at[k - ALT, pl.ds(pl.multiple_of(a * YA + j * G, G), G)],
-            send_sem=s1, recv_sem=q1.at[k], device_id=(b, to), device_id_type=MESH)
+            send_sem=s1.at[0], recv_sem=q1.at[k], device_id=(b, to), device_id_type=MESH)
 
     def e2(k):
         return pltpu.make_async_remote_copy(
             src_ref=y2.at[k - ALT, oth], dst_ref=r2.at[k - ALT],
-            send_sem=s2, recv_sem=q2.at[k], device_id=(ob, a), device_id_type=MESH)
+            send_sem=s2.at[cls(k)], recv_sem=q2.at[k], device_id=(ob, a), device_id_type=MESH)
 
     def e3(k):
         return pltpu.make_async_remote_copy(
             src_ref=r2.at[k - ALT], dst_ref=r3.at[k - ALT],
-            send_sem=s3, recv_sem=q3.at[k], device_id=(ob, a), device_id_type=MESH)
+            send_sem=s3.at[cls(k)], recv_sem=q3.at[k], device_id=(ob, a), device_id_type=MESH)
 
     def e4(k, to):
         return pltpu.make_async_remote_copy(
             src_ref=r1.at[k - ALT, rows(to)], dst_ref=v4.at[a * NM + k - ALT],
-            send_sem=s4, recv_sem=q4, device_id=(b, to), device_id_type=MESH)
-
-    def e4_tail(k, to):
+            send_sem=s4.at[0], recv_sem=q4, device_id=(b, to), device_id_type=MESH)
+
+    def e4_tail(k, n, to):
         return pltpu.make_async_remote_copy(
             src_ref=r1.at[k - ALT, rows(to)], dst_ref=vt_ref.at[a * NTP + k - NM],
-            send_sem=s4, recv_sem=q4t, device_id=(b, to), device_id_type=MESH)
+            send_sem=s4.at[cls(k)], recv_sem=q4t.at[cls(k) * 3 + n], device_id=(b, to), device_id_type=MESH)
 
     gp_own = pltpu.make_async_copy(g_ref.at[b], gp.at[pl.ds(0, H)], gpsem)
 
@@ -211,6 +237,11 @@
         pltpu.make_async_copy(ref, ref, sem).wait()
 
     others = [lax.rem(a + d, NA) for d in (2, 1, 3)]
+    senders = [lax.rem(a + NA - d, NA) for d in (2, 1, 3)]
+
+    gxcopy = pltpu.make_async_remote_copy(
+        src_ref=g_ref.at[KB - 1], dst_ref=gx, send_sem=sgx, recv_sem=qgx,
+        device_id=(b, 3), device_id_type=MESH)
 
     @pl.loop(0, NG)
     def _(j):
@@ -234,6 +265,7 @@
         xs[H:H + 1, yr, H:] = z
         xs[H + 1:, yr, :] = jnp.zeros((NA * KB - H - 1, G, N), F32)
         r1[:, pl.ds(pl.multiple_of(a * YA + j * G, G), G), :] = xs[pl.ds(a * KB + ALT, NP), yr, :]
+        r1[REG - 1 - ALT, pl.ds(pl.multiple_of(a * YA + j * G, G), G), :] = xs[home(a, REG - 1), yr, :]
 
         @pl.when(j + US < NG)
         def _():
@@ -243,6 +275,10 @@
         def _():
             pl.semaphore_wait(barrier, NA)
             gp_other().start()
+
+            @pl.when(a == 1)
+            def _():
+                gxcopy.start()
 
         for k in range(ALT, ALT + EARLY):
             for to in others:
@@ -250,10 +286,20 @@
         for n in range(NA):
             a1(n, j).start()
 
-    @pl.loop(ALT + EARLY, KB)
+    @pl.loop(ALT + EARLY, REG - 1)
     def _(k):
         for to in others:
             e1(k, to).start()
+
+    for to in others:
+        e1(REG - 1, to).start()
+    for k in (REG, REG + 1):
+        for n, to in enumerate(others):
+            @pl.when(used(to, k))
+            def _():
+                e1(k, to, 1 + (k - REG) * 3 + n).start()
+
+    cscopy.wait()
 
     @pl.loop(ALT, ALT + GS)
     def _(k):
@@ -290,6 +336,12 @@
         x = _split(jnp.concatenate([y2[k - ALT, own, :], r2[k - ALT]], axis=1))
         z = _dot6(x, [w3[q] for q in range(3)])
         gcopy(k).wait()
+
+        @pl.when(jnp.logical_and(k == REG - 1, a == 3))
+        def _():
+            gxcopy.wait_recv()
+            gv[(REG - 1) % GS] = gx[...]
+
         gk = gv[lax.rem(k, GS)]
         z = _split(jnp.concatenate([z[:, :N] * gk, z[:, N:] * gk], axis=1))
         z = _dot6(z, [w3i[q] for q in range(3)])
@@ -297,7 +349,7 @@
         r2[k - ALT] = z[:, N:]
         e3(k).start()
 
-        @pl.when(k + GS < KB)
+        @pl.when(k + GS < nk)
         def _():
             gcopy(k + GS).start()
 
@@ -316,8 +368,8 @@
 
         @pl.when(k >= ALT + NM)
         def _():
-            for to in others:
-                e4_tail(k, to).start()
+            for n, to in enumerate(others):
+                e4_tail(k, n, to).start()
             vt_ref[a * NTP + k - NM] = r1[k - ALT, rows(a), :]
 
     def alt_z():
@@ -373,7 +425,7 @@
 
     @pl.loop(ALT, KB + A2 + A3)
     def _(i):
-        @pl.when(i < KB)
+        @pl.when(i < nk)
         def _():
             stage2(i)
 
@@ -382,7 +434,7 @@
             tables()
             alt_z()
 
-        @pl.when(jnp.logical_and(i >= ALT + A2, i < KB + A2))
+        @pl.when(jnp.logical_and(i >= ALT + A2, i < nk + A2))
         def _():
             stage3(i - A2)
 
@@ -399,13 +451,14 @@
             for n in range(NA):
                 a8(n).start()
 
-        @pl.when(i >= ALT + A2 + A3)
+        @pl.when(jnp.logical_and(i >= ALT + A2 + A3, i < nk + A2 + A3))
         def _():
             stage4(i - A2 - A3)
 
         @pl.when(i == I5)
         def _():
             wait_bytes(v4.at[pl.ds(0, (NA - 1) * NM)], q4)
+            t5copy.wait()
 
         @pl.when(i >= I5)
         def _():
@@ -413,17 +466,43 @@
             def _(j):
                 inv_x(j)
 
-    blocks = xs.at[pl.ds(0, (NA - 1) * (KB - ALT))]
-    wait_bytes(blocks, s1)
-    wait_bytes(blocks, s4)
-    wait_bytes(r2, s2)
-    wait_bytes(r2, s3)
+    def blocks(n):
+        return xs.at[pl.ds(0, n)]
+
+    nr = REG - ALT
+    wait_bytes(blocks((NA - 1) * nr), s1.at[0])
+    wait_bytes(blocks((NA - 1) * nr), s4.at[0])
+    wait_bytes(r2.at[pl.ds(0, nr)], s2.at[0])
+    wait_bytes(r2.at[pl.ds(0, nr)], s3.at[0])
+    for k in (REG, REG + 1):
+        c = k - REG + 1
+
+        @pl.when(used(a, k))
+        def _():
+            wait_bytes(blocks(NA - 1), s4.at[c])
+            wait_bytes(r2.at[0], s2.at[c])
+            wait_bytes(r2.at[0], s3.at[c])
+
+        for n in range(NA - 1):
+            @pl.when(used(others[n], k))
+            def _():
+                wait_bytes(xs.at[0], s1.at[1 + (k - REG) * 3 + n])
+
+            @pl.when(used(senders[n], k))
+            def _():
+                wait_bytes(xs.at[0], q4t.at[c * 3 + n])
+
+    @pl.when(a == 1)
+    def _():
+        gxcopy.wait_send()
+
+    for n in range(NA - 1):
+        wait_bytes(blocks(REG - ALT - NM), q4t.at[n])
     wait_bytes(gp.at[pl.ds(0, H)], sg)
     wait_bytes(za, sa1)
     wait_bytes(zs.at[pl.ds(0, NA - 1)], sa3)
     wait_bytes(zs.at[pl.ds(0, NA - 1)], sa6)
     wait_bytes(za, sa8)
-    wait_bytes(xs.at[pl.ds(0, (NTP - ALT) * (NA - 1))], q4t)
     wait_bytes(za, qa8)
 
 
@@ -437,10 +516,11 @@
         vmem = pl.BlockSpec(memory_space=pltpu.VMEM)
         w, vt = pl.pallas_call(
             _k1, name="fwd_yz",
-            in_specs=[vmem, vmem, vmem, any_, any_],
+            in_specs=[vmem, any_, any_, any_, any_],
             out_specs=[vmem, vmem],
             out_shape=[pltpu.VMEM((NG, N, G, H), F32), pltpu.VMEM((NT, YA, N), F32)],
             scratch_shapes=[
+                pltpu.VMEM((3, N, N), BF16), pltpu.VMEM((3, 2, N, N), BF16), pltpu.VMEM((H, N), F32),
                 pltpu.VMEM((US, N, G, H), F32), pltpu.VMEM((NA * NM, YA, N), F32),
                 pltpu.VMEM((NA * KB, YA, N), F32),
                 pltpu.VMEM((NP, N, N), F32), pltpu.VMEM((NP, N, N), F32),
@@ -452,8 +532,10 @@
                 pltpu.VMEM((NA, YA, 2 * N), F32), pltpu.VMEM((N, 2 * N), F32),
                 pltpu.VMEM((N, N), F32), pltpu.VMEM((NA, YA, 2 * N), F32),
                 pltpu.VMEM((NA, YA, N), F32),
-                dma((US,)), dma((GS,)), dma, dma((KB,)), dma, dma((KB,)), dma, dma((KB,)), dma, dma,
-                dma, dma, dma, dma, dma, dma, dma, dma, dma, dma, dma, dma,
+                dma((US,)), dma((GS,)), dma((7,)), dma((KB,)), dma((3,)), dma((KB,)), dma((3,)), dma((KB,)),
+                dma((3,)), dma,
+                dma, dma, dma, dma, dma, dma, dma, dma, dma, dma, dma, dma((9,)),
+                dma((2,)), dma, dma,
             ],
             compiler_params=pltpu.CompilerParams(
                 collective_id=0, has_side_effects=True, vmem_limit_bytes=VM * 2**20),

time: 207 us -> 205 us (level)
    pallas_call x1, Pallas kernels: 201 us -> 199 us  [local(): pl.pallas_call(_k1, name='fwd_yz', in_specs=[vmem, any_, any_, any_, any_...]
where the time goes in v6:
time: 205 us
  Pallas kernels  205 us (100%)
    pallas_call x1, Pallas kernels, local(): pl.pallas_call(_k1, name='fwd_yz', in_specs=[vmem, any_, any_, any_, any_...  199 us
    pallas_call x1, Pallas kernels, local(): pl.pallas_call(_k2, name='inv_x', in_specs=[vmem, vmem, vmem], out_specs=...  5.71 us

profile of v6, /device:TPU:0, one launch (start us, length us, event | category | flops | bytes accessed | tf_op | source)
XLA Modules:
  0.0 204.6 jit_solution(4859960455861574796)
XLA Ops:
  0.0 0.0 copy-start
  0.0 198.8 %fwd_yz.1 = (f32[8,256,8,128]{3,2,1,0:T(8,128)S(1)}, f32[40,64,256]{2,1,0:T(8,128)S(1)}) custom-call(bf16[3,256,256]{2,1,0:T(8,128)(2,1)} %constant.9.clone.t1_ref, bf16[3,256,256]{2,1,0:T(8,128)(2,1)} %constant.10.clone.t5_hbm, bf16[3,2,256,256]{3,2,1,0:T(8,128)(2,1)} %constant.8.clone.cs_hbm, f32[256,64,128]{2,1,0:T(8,128)} %u_ref.1, f32[33,128,256]{2,1,0:T(8,128)} %g_ref.1), custom_call_target="tpu_custom_call" | custom-call | tf_op jit(solution)/shard_map/fwd_yz/pallas_call | solution.py:517
  198.8 0.0 copy-done
  198.8 5.7 %inv_x.1 = f32[256,64,128]{2,1,0:T(8,128)} custom-call(bf16[256,480]{1,0:T(8,128)(2,1)S(1)} %copy-done, f32[8,256,8,128]{3,2,1,0:T(8,128)S(1)} %get-tuple-element.7.w_ref, f32[40,64,256]{2,1,0:T(8,128)S(1)} %get-tuple-element.8.v_ref), custom_call_target="tpu_custom_call" | custom-call | tf_op jit(solution)/shard_map/inv_x/pallas_call | solution.py:543
Async XLA Ops:
  0.0 198.8 %copy-start = (bf16[256,480]{1,0:T(8,128)(2,1)S(1)}, bf16[256,480]{1,0:T(8,128)(2,1)}, u32[]{:S(2)}) copy-start(bf16[256,480]{1,0:T(8,128)(2,1)} %constant.11.clone.t_ref) | copy-start | bytes 737284

commit v7 on v6

--- a/solution.py
+++ b/solution.py
@@ -26,10 +26,13 @@
 NTP = 10
 NM = KB - NTP
 MAIN = np.arange(ALT, ALT + NM)
+MIDS = (2, 3, 4, 5, 6)
+ENDS = (0, 1, 7, 8, 9)
 TAIL = np.concatenate([np.arange(ALT), np.arange(ALT + NM, KB)])
 NT = NA * NTP
 REG = KB - 2
 NP = KB - ALT
+QS = 8
 GS = 6
 I5 = 31
 PG = 3
@@ -66,12 +69,15 @@
     ci = (-s[:, kc] * wgt).astype(np.float32)
     blk = np.arange(NA * KB).reshape(NA, KB)
     main = blk[:, MAIN].ravel()
-    tail = blk[:, TAIL].ravel()
     pad = np.zeros((N, H - main.size), np.float32)
     t5m = np.concatenate([cr[:, main], pad, ci[:, main], pad], 1)
-    t5t = _np_split(np.concatenate([cr[:, tail], ci[:, tail]], 1))
-    t5t = np.concatenate([t5t[i] for i, _ in PAIRS], 1)
-    return cs, _np_split(t1), _np_split(t5m), t5t
+
+    def stack(part):
+        idx = blk[:, TAIL[list(part)]].ravel()
+        t = _np_split(np.concatenate([cr[:, idx], ci[:, idx]], 1))
+        return np.concatenate([t[i] for i, _ in PAIRS], 1)
+
+    return cs, _np_split(t1), _np_split(t5m), stack(MIDS), stack(ENDS)
 
 
 def _split(x):
@@ -81,7 +87,7 @@
     return h, m, (r - m.astype(F32)).astype(BF16)
 
 
-PAIRS = ((0, 0), (0, 1), (1, 0), (1, 1), (0, 2), (2, 0))
+PAIRS = ((0, 0), (1, 0), (2, 0), (0, 1), (1, 1), (0, 2))
 
 
 def _dot6(ls, rs):
@@ -92,6 +98,21 @@
     return acc
 
 
+def _late_part(v_ref, part, yr, tab):
+    def half(lanes):
+        return [v_ref[n * NTP + t:n * NTP + t + 1, yr, lanes] for n in range(NA) for t in part]
+
+    t = jnp.swapaxes(jnp.concatenate(half(slice(0, H)) + half(slice(H, N)), axis=0), 0, 1)
+    outs = []
+    for q in range(G // 2):
+        p = _split(jnp.concatenate([t[2 * q], t[2 * q + 1]], axis=1))
+        p = [x.astype(F32) for x in p]
+        x = jnp.concatenate([p[k] for _, k in PAIRS], axis=0).astype(BF16)
+        acc = jnp.dot(tab, x, preferred_element_type=F32)
+        outs += [acc[:, :H], acc[:, H:]]
+    return jnp.swapaxes(jnp.stack(outs), 0, 1)
+
+
 def _k2(t_ref, w_ref, v_ref, o_ref, buf, osem):
     def yr(j):
         return pl.ds(pl.multiple_of(j * G, G), G)
@@ -101,17 +122,7 @@
 
     @pl.loop(0, NG)
     def _(j):
-        t = jnp.swapaxes(v_ref[:, yr(j), :], 0, 1)
-        outs = []
-        for q in range(G // 2):
-            x = jnp.concatenate([
-                jnp.concatenate([t[2 * q][:, :H], t[2 * q + 1][:, :H]], axis=1),
-                jnp.concatenate([t[2 * q][:, H:], t[2 * q + 1][:, H:]], axis=1)], axis=0)
-            p = _split(x)
-            x = jnp.concatenate([p[k] for _, k in PAIRS], axis=0)
-            acc = jnp.dot(t_ref[...], x, preferred_element_type=F32)
-            outs += [acc[:, :H], acc[:, H:]]
-        buf[j] = w_ref[j] + jnp.swapaxes(jnp.stack(outs), 0, 1)
+        buf[j] = w_ref[j] + _late_part(v_ref, ENDS, yr(j), t_ref[...])
         wr(j).start()
 
     @pl.loop(0, NG)
@@ -119,7 +130,8 @@
         wr(j).wait()
 
 
-def _k1(t1_ref, t5_hbm, cs_hbm, u_ref, g_ref, w_ref, vt_ref, t5_ref, cs_ref, gx, us, v4, xs, r1, y2, r2, r3, gv, w3, w3i, t4,
+def _k1(t1_ref, t5_hbm, t6_hbm, cs_hbm, u_ref, g_ref, w_ref, vt_ref, t5_ref, t6_ref, cs_ref, gx,
+        us, v4, xs, r1, y2, r2, r3, gv, w3, w3i, t4,
         gp, za, zs, ya, fa, zb, vx,
         usem, gsem, s1, q1, s2, q2, s3, q3, s4, q4,
         gpsem, sg, qg, sa1, qa1, sa3, qa3, sa6, qa6, sa8, qa8, q4t,
@@ -144,8 +156,10 @@
 
     cscopy = pltpu.make_async_copy(cs_hbm, cs_ref, tsem.at[0])
     t5copy = pltpu.make_async_copy(t5_hbm, t5_ref, tsem.at[1])
+    t6copy = pltpu.make_async_copy(t6_hbm, t6_ref, tsem.at[2])
     cscopy.start()
     t5copy.start()
+    t6copy.start()
     for n in (2 * NTP - 1, 4 * NTP - 2, 4 * NTP - 1):
         vt_ref[n] = jnp.zeros((YA, N), F32)
 
@@ -188,12 +202,12 @@
     def e2(k):
         return pltpu.make_async_remote_copy(
             src_ref=y2.at[k - ALT, oth], dst_ref=r2.at[k - ALT],
-            send_sem=s2.at[cls(k)], recv_sem=q2.at[k], device_id=(ob, a), device_id_type=MESH)
+            send_sem=s2.at[cls(k)], recv_sem=q2.at[lax.rem(k, QS)], device_id=(ob, a), device_id_type=MESH)
 
     def e3(k):
         return pltpu.make_async_remote_copy(
             src_ref=r2.at[k - ALT], dst_ref=r3.at[k - ALT],
-            send_sem=s3.at[cls(k)], recv_sem=q3.at[k], device_id=(ob, a), device_id_type=MESH)
+            send_sem=s3.at[cls(k)], recv_sem=q3.at[lax.rem(k, QS)], device_id=(ob, a), device_id_type=MESH)
 
     def e4(k, to):
         return pltpu.make_async_remote_copy(
@@ -469,6 +483,14 @@
     def blocks(n):
         return xs.at[pl.ds(0, n)]
 
+    for n in range(NA - 1):
+        wait_bytes(blocks(REG - ALT - NM), q4t.at[n])
+    t6copy.wait()
+
+    @pl.loop(0, NG)
+    def _(j):
+        w_ref[j] += _late_part(vt_ref, MIDS, pl.ds(pl.multiple_of(j * G, G), G), t6_ref[...])
+
     nr = REG - ALT
     wait_bytes(blocks((NA - 1) * nr), s1.at[0])
     wait_bytes(blocks((NA - 1) * nr), s4.at[0])
@@ -496,8 +518,6 @@
     def _():
         gxcopy.wait_send()
 
-    for n in range(NA - 1):
-        wait_bytes(blocks(REG - ALT - NM), q4t.at[n])
     wait_bytes(gp.at[pl.ds(0, H)], sg)
     wait_bytes(za, sa1)
     wait_bytes(zs.at[pl.ds(0, NA - 1)], sa3)
@@ -507,20 +527,21 @@
 
 
 def solution(mesh):
-    cs_np, t1_np, t5m_np, t5t_np = _np_tables()
+    tables = _np_tables()
     dma = pltpu.SemaphoreType.DMA
 
     def local(u, g):
-        cs, t1, t5m, t5t = (jnp.asarray(t) for t in (cs_np, t1_np, t5m_np, t5t_np))
+        cs, t1, t5m, t6, t5t = (jnp.asarray(t) for t in tables)
         any_ = pl.BlockSpec(memory_space=pl.ANY)
         vmem = pl.BlockSpec(memory_space=pltpu.VMEM)
         w, vt = pl.pallas_call(
             _k1, name="fwd_yz",
-            in_specs=[vmem, any_, any_, any_, any_],
+            in_specs=[vmem, any_, any_, any_, any_, any_],
             out_specs=[vmem, vmem],
             out_shape=[pltpu.VMEM((NG, N, G, H), F32), pltpu.VMEM((NT, YA, N), F32)],
             scratch_shapes=[
-                pltpu.VMEM((3, N, N), BF16), pltpu.VMEM((3, 2, N, N), BF16), pltpu.VMEM((H, N), F32),
+                pltpu.VMEM((3, N, N), BF16), pltpu.VMEM((N, 240), BF16),
+                pltpu.VMEM((3, 2, N, N), BF16), pltpu.VMEM((H, N), F32),
                 pltpu.VMEM((US, N, G, H), F32), pltpu.VMEM((NA * NM, YA, N), F32),
                 pltpu.VMEM((NA * KB, YA, N), F32),
                 pltpu.VMEM((NP, N, N), F32), pltpu.VMEM((NP, N, N), F32),
@@ -532,14 +553,14 @@
                 pltpu.VMEM((NA, YA, 2 * N), F32), pltpu.VMEM((N, 2 * N), F32),
                 pltpu.VMEM((N, N), F32), pltpu.VMEM((NA, YA, 2 * N), F32),
                 pltpu.VMEM((NA, YA, N), F32),
-                dma((US,)), dma((GS,)), dma((7,)), dma((KB,)), dma((3,)), dma((KB,)), dma((3,)), dma((KB,)),
+                dma((US,)), dma((GS,)), dma((7,)), dma((KB,)), dma((3,)), dma((QS,)), dma((3,)), dma((QS,)),
                 dma((3,)), dma,
                 dma, dma, dma, dma, dma, dma, dma, dma, dma, dma, dma, dma((9,)),
-                dma((2,)), dma, dma,
+                dma((3,)), dma, dma,
             ],
             compiler_params=pltpu.CompilerParams(
                 collective_id=0, has_side_effects=True, vmem_limit_bytes=VM * 2**20),
-        )(t1, t5m, cs, u, g)
+        )(t1, t5m, t6, cs, u, g)
         return pl.pallas_call(
             _k2, name="inv_x",
             in_specs=[vmem, vmem, vmem], out_specs=any_,

time: 205 us -> 203 us (level)
  no operation moved by 1% of the time
where the time goes in v7:
time: 203 us
  Pallas kernels  203 us (100%)
    pallas_call x1, Pallas kernels, local(): pl.pallas_call(_k1, name='fwd_yz', in_specs=[vmem, any_, any_, any_, any_...  199 us
    pallas_call x1, Pallas kernels, local(): pl.pallas_call(_k2, name='inv_x', in_specs=[vmem, vmem, vmem], out_specs=...  4.34 us

profile of v7, /device:TPU:0, one launch (start us, length us, event | category | flops | bytes accessed | tf_op | source)
XLA Modules:
  0.0 203.3 jit_solution(12887140801028264614)
XLA Ops:
  0.0 0.0 copy-start
  0.0 199.0 %fwd_yz.1 = (f32[8,256,8,128]{3,2,1,0:T(8,128)S(1)}, f32[40,64,256]{2,1,0:T(8,128)S(1)}) custom-call(bf16[3,256,256]{2,1,0:T(8,128)(2,1)} %constant.11.clone.t1_ref, bf16[3,256,256]{2,1,0:T(8,128)(2,1)} %constant.12.clone.t5_hbm, bf16[256,240]{1,0:T(8,128)(2,1)} %constant.13.clone.t6_hbm, bf16[3,2,256,256]{3,2,1,0:T(8,128)(2,1)} %constant.10.clone.cs_hbm, ...), custom_call_target="tpu_custom_call" | custom-call | tf_op jit(solution)/shard_map/fwd_yz/pallas_call | solution.py:537
  199.0 0.0 copy-done
  199.0 4.3 %inv_x.1 = f32[256,64,128]{2,1,0:T(8,128)} custom-call(bf16[256,240]{1,0:T(8,128)(2,1)S(1)} %copy-done, f32[8,256,8,128]{3,2,1,0:T(8,128)S(1)} %get-tuple-element.7.w_ref, f32[40,64,256]{2,1,0:T(8,128)S(1)} %get-tuple-element.8.v_ref), custom_call_target="tpu_custom_call" | custom-call | tf_op jit(solution)/shard_map/inv_x/pallas_call | solution.py:564
Async XLA Ops:
  0.0 199.0 %copy-start = (bf16[256,240]{1,0:T(8,128)(2,1)S(1)}, bf16[256,240]{1,0:T(8,128)(2,1)}, u32[]{:S(2)}) copy-start(bf16[256,240]{1,0:T(8,128)(2,1)} %constant.14.clone.t_ref) | copy-start | bytes 368644

commit v8 on v7

--- a/solution.py
+++ b/solution.py
@@ -130,8 +130,8 @@
         wr(j).wait()
 
 
-def _k1(t1_ref, t5_hbm, t6_hbm, cs_hbm, u_ref, g_ref, w_ref, vt_ref, t5_ref, t6_ref, cs_ref, gx,
-        us, v4, xs, r1, y2, r2, r3, gv, w3, w3i, t4,
+def _k1(t1_hbm, t5_hbm, t6_hbm, cs_hbm, u_ref, g_ref, w_ref, vt_ref, t1_ref, t5_ref, t6_ref,
+        cs_ref, gx, us, v4, xs, r1, y2, r2, r3, gv, w3, w3i, t4,
         gp, za, zs, ya, fa, zb, vx,
         usem, gsem, s1, q1, s2, q2, s3, q3, s4, q4,
         gpsem, sg, qg, sa1, qa1, sa3, qa3, sa6, qa6, sa8, qa8, q4t,
@@ -150,7 +150,11 @@
 
     nk = KB - lax.rem(a, 2) * (1 + a // 3)
 
-    @pl.loop(0, US)
+    ucopy(0).start()
+    t1copy = pltpu.make_async_copy(t1_hbm, t1_ref, tsem.at[3])
+    t1copy.start()
+
+    @pl.loop(1, US)
     def _(j):
         ucopy(j).start()
 
@@ -256,6 +260,8 @@
     gxcopy = pltpu.make_async_remote_copy(
         src_ref=g_ref.at[KB - 1], dst_ref=gx, send_sem=sgx, recv_sem=qgx,
         device_id=(b, 3), device_id_type=MESH)
+
+    t1copy.wait()
 
     @pl.loop(0, NG)
     def _(j):
@@ -536,11 +542,11 @@
         vmem = pl.BlockSpec(memory_space=pltpu.VMEM)
         w, vt = pl.pallas_call(
             _k1, name="fwd_yz",
-            in_specs=[vmem, any_, any_, any_, any_, any_],
+            in_specs=[any_] * 6,
             out_specs=[vmem, vmem],
             out_shape=[pltpu.VMEM((NG, N, G, H), F32), pltpu.VMEM((NT, YA, N), F32)],
             scratch_shapes=[
-                pltpu.VMEM((3, N, N), BF16), pltpu.VMEM((N, 240), BF16),
+                pltpu.VMEM((3, N, N), BF16), pltpu.VMEM((3, N, N), BF16), pltpu.VMEM((N, 240), BF16),
                 pltpu.VMEM((3, 2, N, N), BF16), pltpu.VMEM((H, N), F32),
                 pltpu.VMEM((US, N, G, H), F32), pltpu.VMEM((NA * NM, YA, N), F32),
                 pltpu.VMEM((NA * KB, YA, N), F32),
@@ -556,7 +562,7 @@
                 dma((US,)), dma((GS,)), dma((7,)), dma((KB,)), dma((3,)), dma((QS,)), dma((3,)), dma((QS,)),
                 dma((3,)), dma,
                 dma, dma, dma, dma, dma, dma, dma, dma, dma, dma, dma, dma((9,)),
-                dma((3,)), dma, dma,
+                dma((4,)), dma, dma,
             ],
             compiler_params=pltpu.CompilerParams(
                 collective_id=0, has_side_effects=True, vmem_limit_bytes=VM * 2**20),

time: 203 us -> 203 us (level)
  no operation moved by 1% of the time
where the time goes in v8:
time: 203 us; the launch traced here: 202 us
  Pallas kernels  202 us (100%)
    pallas_call x1, Pallas kernels, local(): pl.pallas_call(_k1, name='fwd_yz', in_specs=[any_] * 6, out_specs=[vmem,...  198 us
    pallas_call x1, Pallas kernels, local(): pl.pallas_call(_k2, name='inv_x', in_specs=[vmem, vmem, vmem], out_specs=...  4.34 us

profile of v8, /device:TPU:0, one launch (start us, length us, event | category | flops | bytes accessed | tf_op | source)
XLA Modules:
  0.0 202.4 jit_solution(13761699800016507855)
XLA Ops:
  0.0 0.0 copy-start
  0.0 198.1 %fwd_yz.1 = (f32[8,256,8,128]{3,2,1,0:T(8,128)S(1)}, f32[40,64,256]{2,1,0:T(8,128)S(1)}) custom-call(bf16[3,256,256]{2,1,0:T(8,128)(2,1)} %constant.11.clone.t1_hbm, bf16[3,256,256]{2,1,0:T(8,128)(2,1)} %constant.12.clone.t5_hbm, bf16[256,240]{1,0:T(8,128)(2,1)} %constant.13.clone.t6_hbm, bf16[3,2,256,256]{3,2,1,0:T(8,128)(2,1)} %constant.10.clone.cs_hbm, ...), custom_call_target="tpu_custom_call" | custom-call | tf_op jit(solution)/shard_map/fwd_yz/pallas_call | solution.py:543
  198.1 0.0 copy-done
  198.1 4.3 %inv_x.1 = f32[256,64,128]{2,1,0:T(8,128)} custom-call(bf16[256,240]{1,0:T(8,128)(2,1)S(1)} %copy-done, f32[8,256,8,128]{3,2,1,0:T(8,128)S(1)} %get-tuple-element.7.w_ref, f32[40,64,256]{2,1,0:T(8,128)S(1)} %get-tuple-element.8.v_ref), custom_call_target="tpu_custom_call" | custom-call | tf_op jit(solution)/shard_map/inv_x/pallas_call | solution.py:570
Async XLA Ops:
  0.0 198.1 %copy-start = (bf16[256,240]{1,0:T(8,128)(2,1)S(1)}, bf16[256,240]{1,0:T(8,128)(2,1)}, u32[]{:S(2)}) copy-start(bf16[256,240]{1,0:T(8,128)(2,1)} %constant.14.clone.t_ref) | copy-start | bytes 368644
